TPU v7x, 128 devices: a whole 4x4x4 slice. The times are simulated.
128 devices in a mesh: ep: 4 (over z), fsdp: 32 (over y, x, core).
Axes of the slice: x: 4, y: 4, z: 4, core: 2. Of those that a mesh axis runs over, the one named last changes fastest.
Arguments:
- train_gate: float32 [64, 2048, 1408], P('ep', 'fsdp'), may hold values from -0.25 to 0.25
- train_up: float32 [64, 2048, 1408], P('ep', 'fsdp'), may hold values from -0.25 to 0.25
- train_down: float32 [64, 1408, 2048], P('ep', None, 'fsdp'), may hold values from -0.3125 to 0.3125
- router_weight: float32 [2048, 64], P('fsdp', 'ep'), may hold values from -0.125 to 0.125
- router_gain: float32 [2048], P('fsdp'), may hold values from 0.25 to 1.75
Outputs:
- ready_gate: bfloat16 [64, 2048, 1408], P('ep', None, 'fsdp')
- ready_up: bfloat16 [64, 2048, 1408], P('ep', None, 'fsdp')
- ready_down: bfloat16 [64, 1408, 2048], P('ep', 'fsdp')
- scale_gate: float32 [64, 1408], P('ep', 'fsdp')
- scale_up: float32 [64, 1408], P('ep', 'fsdp')
- scale_down: float32 [64, 1408], P('ep', 'fsdp')
- serve_router: bfloat16 [2048, 64], replicated
All inputs are finite; a program needn't handle non-finite values.
Results may differ from a plain program's by a relative error of at most 0.001.
Values may be sent and summed in bfloat16 or wider, within the bound.
No kernel may reach another device: no remote copies, remote signals or barrier semaphores. Data moves between devices by JAX's collectives and lax.ppermute only.
A program may use at most 192 MiB of HBM per device.

v0:
```python
import functools

import jax
import jax.numpy as jnp
from jax import lax
from jax.experimental import pallas as pl
from jax.experimental.pallas import tpu as pltpu
from jax.sharding import Mesh, PartitionSpec as P


POWER = 17
REACH = 180.0
FLOOR = 1e-37
LANES = 128
HALF = LANES // 2
STEP = 4
SIDE = 4
PLANE = ("y", "x", "core")
SHIFTS = (
    (1, 0), (3, 0), (0, 1), (0, 3), (1, 1), (3, 3), (1, 3), (3, 1),
    (2, 0), (0, 2), (2, 1), (2, 3), (1, 2), (3, 2), (2, 2),
)


def anywhere(count):
    return [pl.BlockSpec(memory_space=pl.ANY)] * count


def rows_at(start, size, unit):
    return pl.ds(pl.multiple_of(start, unit), size)


def landed(ref, sem):
    pltpu.make_async_copy(ref, ref, sem).wait()


def chip_at(dx, dy):
    y, x = lax.axis_index("y"), lax.axis_index("x")
    return lax.rem(y + dy, SIDE) * SIDE + lax.rem(x + dx, SIDE)


def behind(ahead, kernel):
    return lambda *refs: kernel(*refs[ahead:])


def encode_tiles(x, xin, stage, pay, sums, notes, sem_in, peers, tiles, after):
    depth, experts, _, _ = xin.shape
    half = experts // 2
    share = tiles * LANES // peers
    odd = lax.axis_index("core")

    def fetch(i):
        slot = lax.rem(i, depth)
        at = rows_at(i * LANES, LANES, LANES)
        pltpu.make_async_copy(x.at[:, :, at], xin.at[slot], sem_in.at[slot]).start()

    def first(i, carry):
        fetch(i)
        return carry

    lax.fori_loop(0, depth, first, 0)

    def tile_of(i, carry):
        slot = lax.rem(i, depth)
        landed(xin.at[slot], sem_in.at[slot])
        at = rows_at(i * LANES, LANES, LANES)
        for e in range(half):
            a, b = xin[slot, e + half * odd], xin[slot, e + half * (1 - odd)]
            sa = jnp.sum(a * a, 0, keepdims=True)
            sb = jnp.sum(b * b, 0, keepdims=True)
            sums[pl.ds(e, 1), at] = sa
            sums[pl.ds(e + half, 1), at] = sb
            a = a * (REACH * lax.rsqrt(jnp.maximum(sa, FLOOR)))
            b = b * (REACH * lax.rsqrt(jnp.maximum(sb, FLOOR)))
            v = jnp.concatenate([a, b], 0)
            v2 = v * v
            v4 = v2 * v2
            v8 = v4 * v4
            y = v8 * v8 * v
            stage[pl.ds(e, LANES, stride=half), :] = y.T
        pay[rows_at(i * LANES * half, LANES * half, LANES * half), :] = stage[...].astype(jnp.bfloat16)

        @pl.when(i + depth < tiles)
        def _():
            fetch(i + depth)

        after(i)
        return carry

    lax.fori_loop(0, tiles, tile_of, 0)
    total = sums[...]
    total = jnp.where(odd == 1, jnp.concatenate([total[half:], total[:half]], 0), total)
    high = total.astype(jnp.bfloat16).astype(jnp.float32)
    low = total - high
    gap = jnp.zeros((experts, HALF - share), jnp.float32)
    for d in range(peers):
        piece = slice(d * share, (d + 1) * share)
        notes[d] = jnp.concatenate([high[:, piece], gap, low[:, piece], gap], 1).astype(jnp.bfloat16)


def encode_scratch(peers, experts, rows, columns, depth):
    return [
        pltpu.VMEM((depth, experts, rows, LANES), jnp.float32),
        pltpu.VMEM((LANES * experts // 2, LANES), jnp.float32),
        pltpu.VMEM((columns * experts // 2, LANES), jnp.bfloat16),
        pltpu.VMEM((experts, columns), jnp.float32),
        pltpu.VMEM((peers, experts, LANES), jnp.bfloat16),
        pltpu.SemaphoreType.DMA((depth,)),
        pltpu.SemaphoreType.DMA,
        pltpu.SemaphoreType.DMA,
    ]


def encode_bulk_kernel(routed, peers, tiles, *refs):
    x, out = refs[0], refs[1 + 2 * routed]
    xin, stage, pay, sums, notes, sem_in, sem_pay, sem_note = refs[2 + 2 * routed : 10 + 2 * routed]
    experts = xin.shape[1]
    half = experts // 2
    share = tiles * LANES // peers
    block = share * half

    if routed:
        weight, gain = refs[1:3]
        router, sem_router = refs[10 + 2 * routed :]
        part = weight[...] * gain[...]
        part = jnp.where(lax.axis_index("core") == 1, jnp.concatenate([part[half:], part[:half]], 0), part)
        part = jnp.concatenate([part[:half], part[half:]], 1)
        part = jnp.concatenate([part, jnp.zeros_like(part)], 0).astype(jnp.bfloat16)
        for d in range(peers):
            router[d] = part
        pltpu.make_async_copy(router, out.at[:, pl.ds(block + experts, experts), :], sem_router).start()

    def after(tile):
        def send(d, inner):
            pltpu.make_async_copy(
                pay.at[rows_at(d * block, block, 16), :], out.at[d, pl.ds(0, block), :], sem_pay
            ).start()
            return inner

        lax.fori_loop(tile * LANES // share, (tile + 1) * LANES // share, send, 0)

    encode_tiles(x, xin, stage, pay, sums, notes, sem_in, peers, tiles, after)
    pltpu.make_async_copy(notes, out.at[:, pl.ds(block, experts), :], sem_note).start()
    landed(pay, sem_pay)
    landed(notes, sem_note)
    if routed:
        landed(router, sem_router)


def encode_bulk(x, small, ahead, peers, depth=8):
    experts, rows, columns = x.shape
    routed = len(small) // 2
    height = columns // peers * experts // 2 + experts * (1 + routed)
    return pl.pallas_call(
        behind(len(ahead), functools.partial(encode_bulk_kernel, routed, peers, columns // LANES)),
        in_specs=anywhere(len(ahead) + 1) + [pl.BlockSpec(memory_space=pltpu.VMEM)] * len(small),
        out_specs=pl.BlockSpec(memory_space=pl.ANY),
        out_shape=jax.ShapeDtypeStruct((peers, height, LANES), jnp.bfloat16),
        scratch_shapes=encode_scratch(peers, experts, rows, columns, depth)
        + [pltpu.VMEM((peers, experts, LANES), jnp.bfloat16), pltpu.SemaphoreType.DMA] * routed,
        name="encode_bulk",
    )(*ahead, x, *small)


def encode_head_kernel(peers, tiles, x, keep, give, *scratch):
    xin, stage, pay, sums, notes, sem_in, sem_pay, sem_note = scratch
    experts = xin.shape[1]
    block = tiles * LANES // peers * experts // 2
    core = lax.axis_index("core")
    encode_tiles(x, xin, stage, pay, sums, notes, sem_in, peers, tiles, lambda tile: None)
    for k, (dx, dy) in enumerate(((0, 0),) + SHIFTS):
        chip = chip_at(dx, dy)
        for out, which in ((give, 1 - core), (keep, core)):
            d = 2 * chip + which
            pltpu.make_async_copy(
                pay.at[rows_at(d * block, block, 16), :], out.at[k, pl.ds(0, block), :], sem_pay
            ).start()
            pltpu.make_async_copy(notes.at[d], out.at[k, pl.ds(block, experts), :], sem_note).start()
    landed(pay, sem_pay)
    landed(notes, sem_note)


def encode_head(x, ahead, peers, depth=8):
    experts, rows, columns = x.shape
    height = columns // peers * experts // 2 + experts
    return pl.pallas_call(
        behind(len(ahead), functools.partial(encode_head_kernel, peers, columns // LANES)),
        in_specs=anywhere(len(ahead) + 1),
        out_specs=anywhere(2),
        out_shape=[jax.ShapeDtypeStruct((len(SHIFTS) + 1, height, LANES), jnp.bfloat16)] * 2,
        scratch_shapes=encode_scratch(peers, experts, rows, columns, depth),
        name="encode_head",
    )(*ahead, x)


def pair_kernel(keep, got, *refs):
    outs, (held, sem_in, sem_out) = refs[: len(SHIFTS) + 1], refs[len(SHIFTS) + 1 :]
    for k, a in enumerate((keep, got)):
        pltpu.make_async_copy(a, held.at[k], sem_in.at[k]).start()
    for k in range(2):
        landed(held.at[k], sem_in.at[k])
    for i, out in enumerate(outs):
        pltpu.make_async_copy(held.at[:, i], out, sem_out).start()
    landed(held, sem_out)


def paired(keep, got):
    count, height, _ = keep.shape
    return pl.pallas_call(
        pair_kernel,
        in_specs=anywhere(2),
        out_specs=anywhere(count),
        out_shape=[jax.ShapeDtypeStruct((2, height, LANES), jnp.bfloat16)] * count,
        scratch_shapes=[
            pltpu.VMEM((2, count, height, LANES), jnp.bfloat16),
            pltpu.SemaphoreType.DMA((2,)),
            pltpu.SemaphoreType.DMA,
        ],
        name="paired",
    )(keep, got)


def two_cores(a, b):
    left = lax.broadcasted_iota(jnp.int32, a.shape, 1) < HALF
    return jnp.concatenate([jnp.where(left, a, b), pltpu.roll(jnp.where(left, b, a), HALF, 1)], 0)


def decode_kernel(share, depth, head, routed, *refs):
    sources, refs = refs[:head] if head else refs[:1], refs[max(head, 1) :]
    ready_out, scale_out, refs = refs[0], refs[1], refs[2:]
    router, refs = (refs[0], refs[1:]) if routed else (None, refs)
    pay, notes, factors, turned, ready_factors, picks, ready, sem_in, sem_note, sem_out = refs
    chips, _, experts = notes.shape[1:4]
    half = experts // 2
    height = STEP * half
    steps = share // STEP
    outs = ready.shape[0]
    block = share * half

    def fetch(i):
        slot = lax.rem(i, depth)
        pltpu.make_async_copy(
            sources[0].at[:, :, rows_at(i * height, height, height), :], pay.at[slot], sem_in.at[slot]
        ).start()

    if head:
        core = lax.axis_index("core")
        for source, (dx, dy) in zip(sources, ((0, 0),) + SHIFTS):
            chip = chip_at(SIDE - dx, SIDE - dy)
            for k, which in enumerate((core, 1 - core)):
                pltpu.make_async_copy(
                    source.at[k, pl.ds(block, experts)], notes.at[0, chip, which], sem_note.at[0]
                ).start()
                pltpu.make_async_copy(source.at[k, pl.ds(0, block)], pay.at[0, chip, which], sem_in.at[0]).start()
    else:
        for k in range(1 + routed):
            rows = pl.ds(block + k * experts, experts)
            pltpu.make_async_copy(sources[0].at[:, :, rows, :], notes.at[k], sem_note.at[k]).start()

        def first(i, carry):
            fetch(i)
            return carry

        lax.fori_loop(0, depth, first, 0)

    copies = 3
    row = lax.broadcasted_iota(jnp.int32, (LANES, LANES), 0)
    right = jnp.where(lax.broadcasted_iota(jnp.int32, (LANES, LANES), 1) < HALF, 0, 1)
    peer = jnp.where(row < copies * 2 * chips, lax.rem(row, 2 * chips), -1)
    for q in range(chips):
        picks[:, q * LANES : (q + 1) * LANES] = jnp.where(peer == 2 * q + right, 1.0, 0.0).astype(jnp.bfloat16)

    def plain(code):
        y = code.astype(jnp.float32)
        size = jnp.maximum(jnp.abs(y), 1.2e-38)
        return y * jnp.exp2(jnp.log2(size) * (1.0 / POWER - 1.0))

    if routed:
        landed(notes.at[1], sem_note.at[1])
        for q in range(chips):
            a, b = (notes[1, q, c].astype(jnp.float32)[:half] for c in range(2))
            router[:, q * LANES : (q + 1) * LANES] = two_cores(a, b).astype(jnp.bfloat16)

    landed(notes.at[0], sem_note.at[0])
    part = notes[0].astype(jnp.float32).reshape(2 * chips, experts, LANES)
    part = part + pltpu.roll(part, HALF, 2)
    scale = jnp.sqrt(jnp.sum(part, 0))
    scale_out[...] = scale[:, :share]
    part = jnp.sqrt(jnp.maximum(part, FLOOR)) * (1.0 / (REACH * scale))[None]
    factors[...] = part.reshape(2 * chips * experts, LANES)
    tall = ready_factors.shape[0] // experts
    for e in range(experts):
        value = factors[pl.ds(e, 2 * chips, stride=experts), :]
        pieces = []
        for _ in range(copies):
            pieces.append(value.astype(jnp.bfloat16).astype(jnp.float32))
            value = value - pieces[-1]
        pieces.append(jnp.zeros((LANES - copies * 2 * chips, LANES), jnp.float32))
        turned[pl.ds(e, tall, stride=experts), :] = jnp.concatenate(pieces, 0).T[:tall]
    ready_factors[...] = turned[...].astype(jnp.bfloat16)
    if head:
        landed(pay, sem_in.at[0])

    def step_of(s, carry):
        out_slot = lax.rem(s, outs)
        if head:
            slot, base = 0, s * height
        else:
            slot, base = lax.rem(s, depth), 0
            landed(pay.at[slot], sem_in.at[slot])

        @pl.when(s >= outs)
        def _():
            landed(ready.at[out_slot], sem_out.at[out_slot])

        known = ready_factors[rows_at(s * STEP * experts, STEP * experts, STEP * experts), :]
        for q in range(chips):
            if q % 2 == 0:
                wide = picks[:, q * LANES : (q + 2) * LANES]
                factor = jnp.dot(known, wide, preferred_element_type=jnp.float32)
            mine = factor[:, q % 2 * LANES : (q % 2 + 1) * LANES]
            for p in range(STEP // 2):
                rows = rows_at(base + 2 * half * p, 2 * half, 2 * half)
                a2, b2 = (plain(pay[slot, q, c, rows, :]) for c in range(2))
                for h in range(2):
                    j = 2 * p + h
                    value = two_cores(a2[half * h : half * (h + 1)], b2[half * h : half * (h + 1)])
                    value = value * mine[experts * j : experts * (j + 1)]
                    ready[out_slot, j, :, q * LANES : (q + 1) * LANES] = value.astype(jnp.bfloat16)

        if not head:

            @pl.when(s + depth < steps)
            def _():
                fetch(s + depth)

        pltpu.make_async_copy(ready.at[out_slot], ready_out.at[pl.ds(s * STEP, STEP)], sem_out.at[out_slot]).start()
        return carry

    lax.fori_loop(0, steps, step_of, 0)
    for slot in range(outs):
        landed(ready.at[slot], sem_out.at[slot])


def decode(sources, experts, share, rows, routed, depth=8, outs=6):
    head = len(sources) if len(sources) > 1 else 0
    chips = head or sources[0].shape[0]
    half = experts // 2
    tall = -(-share // 8) * 8
    depth, high = (1, share * half) if head else (depth, STEP * half)
    vmem = pl.BlockSpec(memory_space=pltpu.VMEM)
    return pl.pallas_call(
        functools.partial(decode_kernel, share, depth, head, routed),
        in_specs=anywhere(len(sources)),
        out_specs=anywhere(1) + [vmem] * (1 + routed),
        out_shape=[
            jax.ShapeDtypeStruct((share, experts, rows * 2 * chips), jnp.bfloat16),
            jax.ShapeDtypeStruct((experts, share), jnp.float32),
        ]
        + [jax.ShapeDtypeStruct((experts, rows * 2 * chips), jnp.bfloat16)] * routed,
        scratch_shapes=[
            pltpu.VMEM((depth, chips, 2, high, LANES), jnp.bfloat16),
            pltpu.VMEM((1 + routed, chips, 2, experts, LANES), jnp.bfloat16),
            pltpu.VMEM((2 * chips * experts, LANES), jnp.float32),
            pltpu.VMEM((tall * experts, LANES), jnp.float32),
            pltpu.VMEM((tall * experts, LANES), jnp.bfloat16),
            pltpu.VMEM((LANES, chips * LANES), jnp.bfloat16),
            pltpu.VMEM((outs, STEP, experts, rows * 2 * chips), jnp.bfloat16),
            pltpu.SemaphoreType.DMA((depth,)),
            pltpu.SemaphoreType.DMA((1 + routed,)),
            pltpu.SemaphoreType.DMA((outs,)),
        ],
        name="decode_head" if head else "decode_bulk",
    )(*sources)


def moved(value, dx, dy):
    pairs = []
    for y in range(SIDE):
        for x in range(SIDE):
            to = (y + dy) % SIDE * SIDE + (x + dx) % SIDE
            pairs += [(2 * (y * SIDE + x) + core, 2 * to + core) for core in range(2)]
    return lax.ppermute(value, PLANE, pairs)


def body(train_gate, train_up, train_down, router_weight, router_gain):
    peers = lax.axis_size(PLANE)
    experts, rows, columns = train_gate.shape
    share = columns // peers

    def bulk_decoded(arrived, routed):
        return decode((arrived.reshape(peers // 2, 2, *arrived.shape[1:]),), experts, share, rows, routed)

    first = encode_bulk(train_up, (router_weight.T, router_gain[None]), (), peers)
    arrived_first = lax.all_to_all(first, PLANE, 0, 0, tiled=True)
    keep, give = encode_head(train_gate, (first,), peers)
    got = lax.ppermute(give, "core", ((0, 1), (1, 0)))
    second = encode_bulk(jnp.swapaxes(train_down, 1, 2), (), (keep,), peers)
    arrived = list(paired(keep, got))
    for k, shift in enumerate(SHIFTS):
        arrived[k + 1] = moved(arrived[k + 1], *shift)
    arrived_second = lax.all_to_all(second, PLANE, 0, 0, tiled=True)
    up, scale_up, router = bulk_decoded(arrived_first, 1)
    router = lax.all_gather(router, "ep", axis=0, tiled=True)
    gate, scale_gate = decode(tuple(arrived), experts, share, rows, 0)
    down, scale_down = bulk_decoded(arrived_second, 0)
    return (
        jnp.transpose(gate, (1, 2, 0)),
        jnp.transpose(up, (1, 2, 0)),
        jnp.transpose(down, (1, 0, 2)),
        scale_gate,
        scale_up,
        scale_down,
        router.T,
    )


def solution(mesh):
    fine = Mesh(mesh.devices.reshape(mesh.devices.shape[0], SIDE, SIDE, 2), ("ep",) + PLANE)
    return jax.shard_map(
        body,
        mesh=fine,
        in_specs=(
            P("ep", PLANE, None),
            P("ep", PLANE, None),
            P("ep", None, PLANE),
            P(PLANE, "ep"),
            P(PLANE),
        ),
        out_specs=(
            P("ep", None, PLANE),
            P("ep", None, PLANE),
            P("ep", PLANE, None),
            P("ep", PLANE),
            P("ep", PLANE),
            P("ep", PLANE),
            P(),
        ),
        check_vma=False,
    )
```

profile of v0, /device:TPU:14, one launch (start us, length us, event | category | flops | bytes accessed | tf_op | source)
XLA Modules:
  0.0 186.8 jit_solution(7489766608158566977)
XLA Ops:
  0.6 6.0 %encode_bulk.2.refs_0_ = bf16[32,384,128]{2,1,0:T(8,128)(2,1)} custom-call(f32[16,64,1408]{2,1,0:T(8,128)} %refs_0_.1, f32[16,64]{1,0:T(8,128)} %bitcast.13, f32[1,64]{1,0:T(1,128)} %bitcast.14), custom_call_target="tpu_custom_call" | custom-call | tf_op jit(solution)/shard_map/encode_bulk/pallas_call | solution.py:154
  6.7 5.9 %encode_head.1 = (bf16[16,368,128]{2,1,0:T(8,128)(2,1)}, bf16[16,368,128]{2,1,0:T(8,128)(2,1)}) custom-call(bf16[32,384,128]{2,1,0:T(8,128)(2,1)} %encode_bulk.2.refs_0_, f32[16,64,1408]{2,1,0:T(8,128)} %refs_1_.1), custom_call_target="tpu_custom_call" | custom-call | tf_op jit(solution)/shard_map/encode_head/pallas_call | solution.py:186
  12.5 5.2 %encode_bulk.3 = bf16[32,368,128]{2,1,0:T(8,128)(2,1)} custom-call(bf16[16,368,128]{2,1,0:T(8,128)(2,1)} %get-tuple-element.32.keep.refs_0_, f32[16,64,1408]{2,1,0:T(8,128)} %bitcast.11), custom_call_target="tpu_custom_call" | custom-call | tf_op jit(solution)/shard_map/encode_bulk/pallas_call | solution.py:154
  17.7 42.9 %all_to_all.10 = bf16[32,368,128]{2,1,0:T(8,128)(2,1)} all-to-all(bf16[32,368,128]{2,1,0:T(8,128)(2,1)} %encode_bulk.3), channel_id=1, replica_groups=mesh['ep'=4,'y'=4,'x'=4,'core'=2] {'y','x','core'}, dimensions={0} | all-to-all | bytes 6029312 | tf_op jit(solution)/shard_map/all_to_all | solution.py:402
  60.6 7.0 %all-to-all-start = ((bf16[32,384,128]{2,1,0:T(8,128)(2,1)}), bf16[32,384,128]{2,1,0:T(8,128)(2,1)S(1)}, u32[]{:S(2)}, u32[]{:S(2)}) async-start(bf16[32,384,128]{2,1,0:T(8,128)(2,1)} %encode_bulk.2.refs_0_), calls=%async_computation | async-start | bytes 6291456 | tf_op jit(solution)/shard_map/all_to_all | solution.py:395
  67.6 0.2 collective-permute-start
  67.8 3.5 %collective-permute-done.got = bf16[16,368,128]{2,1,0:T(8,128)(2,1)} collective-permute-done((bf16[16,368,128]{2,1,0:T(8,128)(2,1)}, bf16[16,368,128]{2,1,0:T(8,128)(2,1)}, u32[]{:S(2)}, u32[]{:S(2)}) %collective-permute-start) | collective-permute-done | bytes 1507360 | tf_op jit(solution)/shard_map/ppermute | solution.py:397
  71.4 3.5 %paired.1 = (bf16[2,368,128]{2,1,0:T(8,128)(2,1)}, bf16[2,368,128]{2,1,0:T(8,128)(2,1)}, bf16[2,368,128]{2,1,0:T(8,128)(2,1)}, bf16[2,368,128]{2,1,0:T(8,128)(2,...) custom-call(bf16[16,368,128]{2,1,0:T(8,128)(2,1)} %get-tuple-element, ...), custom_call_target="tpu_custom_call" | custom-call | tf_op jit(solution)/shard_map/paired/pallas_call | solution.py:209
  74.8 0.6 collective-permute-start.1
  75.4 1.5 collective-permute-start.2
  76.9 1.5 collective-permute-start.3
  78.4 0.5 collective-permute-start.4
  79.0 2.7 %collective-permute-start.5 = (bf16[2,368,128]{2,1,0:T(8,128)(2,1)}, bf16[2,368,128]{2,1,0:T(8,128)(2,1)}, u32[]{:S(2)}, u32[]{:S(2)}) collective-permute-start(bf16[2,368,128]{2,1,0:T(8,128)(2,1)} %get-tuple-element.39), channel_id=1, source_target_pairs={{0,10},{1,11},{2,12},{3,13},{4,14},{5,15},{6,8},{7,9},{8,18},{9,19... | collective-permute-start | bytes 565256 | tf_op jit(solution)/shard_map/ppermute | solution.py:383
  81.6 28.5 %collective-permute-done.1.refs_1_ = bf16[2,368,128]{2,1,0:T(8,128)(2,1)S(1)} collective-permute-done((bf16[2,368,128]{2,1,0:T(8,128)(2,1)}, bf16[2,368,128]{2,1,0:T(8,128)(2,1)S(1)}, u32[]{:S(2)}, u32[]{:S(2)}) %collective-permute-start.1) | collective-permute-done | bytes 188448 | tf_op jit(solution)/shard_map/ppermute | solution.py:383
  110.2 0.0 copy-start.1
  110.2 0.0 collective-permute-start.6
  110.2 0.0 collective-permute-done.2.refs_2_
  110.2 0.0 copy-start.2
  110.2 5.3 %collective-permute-start.7 = (bf16[2,368,128]{2,1,0:T(8,128)(2,1)}, bf16[2,368,128]{2,1,0:T(8,128)(2,1)}, u32[]{:S(2)}, u32[]{:S(2)}) collective-permute-start(bf16[2,368,128]{2,1,0:T(8,128)(2,1)} %get-tuple-element.41), channel_id=1, source_target_pairs={{0,26},{1,27},{2,28},{3,29},{4,30},{5,31},{6,24},{7,25},{8,2},{9,3... | collective-permute-start | bytes 565256 | tf_op jit(solution)/shard_map/ppermute | solution.py:383
  115.5 0.0 collective-permute-done.3.refs_3_
  115.5 0.0 collective-permute-start.8
  115.5 0.0 collective-permute-done.4.refs_4_
  115.5 0.4 collective-permute-start.9
  115.9 0.0 collective-permute-done.5.refs_5_
  115.9 3.2 %collective-permute-start.10 = (bf16[2,368,128]{2,1,0:T(8,128)(2,1)}, bf16[2,368,128]{2,1,0:T(8,128)(2,1)}, u32[]{:S(2)}, u32[]{:S(2)}) collective-permute-start(bf16[2,368,128]{2,1,0:T(8,128)(2,1)} %get-tuple-element.44), channel_id=1, source_target_pairs={{0,16},{1,17},{2,18},{3,19},{4,20},{5,21},{6,22},{7,23},{8,24},{9,... | collective-permute-start | bytes 565256 | tf_op jit(solution)/shard_map/ppermute | solution.py:383
  119.1 2.2 %collective-permute-done.6.refs_6_ = bf16[2,368,128]{2,1,0:T(8,128)(2,1)} collective-permute-done((bf16[2,368,128]{2,1,0:T(8,128)(2,1)}, bf16[2,368,128]{2,1,0:T(8,128)(2,1)}, u32[]{:S(2)}, u32[]{:S(2)}) %collective-permute-start.6) | collective-permute-done | bytes 188448 | tf_op jit(solution)/shard_map/ppermute | solution.py:383
  121.3 0.0 collective-permute-start.11
  121.3 0.8 collective-permute-done.7.refs_7_
  122.1 3.6 %collective-permute-start.12 = (bf16[2,368,128]{2,1,0:T(8,128)(2,1)}, bf16[2,368,128]{2,1,0:T(8,128)(2,1)}, u32[]{:S(2)}, u32[]{:S(2)}) collective-permute-start(bf16[2,368,128]{2,1,0:T(8,128)(2,1)} %get-tuple-element.46), channel_id=1, source_target_pairs={{0,28},{1,29},{2,30},{3,31},{4,24},{5,25},{6,26},{7,27},{8,4},{9,5... | collective-permute-start | bytes 565256 | tf_op jit(solution)/shard_map/ppermute | solution.py:383
  125.7 10.5 %collective-permute-done.8.refs_8_ = bf16[2,368,128]{2,1,0:T(8,128)(2,1)} collective-permute-done((bf16[2,368,128]{2,1,0:T(8,128)(2,1)}, bf16[2,368,128]{2,1,0:T(8,128)(2,1)}, u32[]{:S(2)}, u32[]{:S(2)}) %collective-permute-start.8) | collective-permute-done | bytes 188448 | tf_op jit(solution)/shard_map/ppermute | solution.py:383
  136.2 0.0 collective-permute-start.13
  136.2 0.0 collective-permute-done.9.refs_9_
  136.2 4.4 %collective-permute-start.14 = (bf16[2,368,128]{2,1,0:T(8,128)(2,1)}, bf16[2,368,128]{2,1,0:T(8,128)(2,1)}, u32[]{:S(2)}, u32[]{:S(2)}) collective-permute-start(bf16[2,368,128]{2,1,0:T(8,128)(2,1)} %get-tuple-element.48), channel_id=1, source_target_pairs={{0,22},{1,23},{2,16},{3,17},{4,18},{5,19},{6,20},{7,21},{8,30},{9,... | collective-permute-start | bytes 565256 | tf_op jit(solution)/shard_map/ppermute | solution.py:383
  140.6 0.0 collective-permute-done.10.refs_10_
  140.6 0.0 collective-permute-start.15
  140.6 0.0 collective-permute-done.11.refs_11_
  140.6 0.0 collective-permute-done.12.refs_12_
  140.7 8.0 %collective-permute-done.13.refs_13_ = bf16[2,368,128]{2,1,0:T(8,128)(2,1)} collective-permute-done((bf16[2,368,128]{2,1,0:T(8,128)(2,1)}, bf16[2,368,128]{2,1,0:T(8,128)(2,1)}, u32[]{:S(2)}, u32[]{:S(2)}) %collective-permute-start.13) | collective-permute-done | bytes 188448 | tf_op jit(solution)/shard_map/ppermute | solution.py:383
  148.6 3.7 %collective-permute-done.14.refs_14_ = bf16[2,368,128]{2,1,0:T(8,128)(2,1)} collective-permute-done((bf16[2,368,128]{2,1,0:T(8,128)(2,1)}, bf16[2,368,128]{2,1,0:T(8,128)(2,1)}, u32[]{:S(2)}, u32[]{:S(2)}) %collective-permute-start.14) | collective-permute-done | bytes 188448 | tf_op jit(solution)/shard_map/ppermute | solution.py:383
  152.4 0.0 collective-permute-done.15.refs_15_
  152.4 0.0 copy-done.1
  152.4 0.0 copy-done.2
  152.4 6.6 %decode_head.1 = (bf16[44,16,2048]{2,1,0:T(8,128)(2,1)}, f32[16,44]{1,0:T(8,128)}) custom-call(bf16[2,368,128]{2,1,0:T(8,128)(2,1)} %get-tuple-element.34.refs_0_, bf16[2,368,128]{2,1,0:T(8,128)(2,1)} %copy-done.1, bf16[2,368,128]{2,1,0:T(8,128)(2,1)} %copy-done.2, bf16[2,368,128]{2,1,0:T(8,128)(2,1)} %collective-permute-done.3.refs_3_, ...), custom_call_target="tpu_custom_call" | custom-call | tf_op jit(solution)/shard_map/decode_head/pallas_call | solution.py:352
  159.0 5.7 %decode_bulk.3 = (bf16[44,16,2048]{2,1,0:T(8,128)(2,1)}, f32[16,44]{1,0:T(8,128)}) custom-call(bf16[16,2,368,128]{3,2,1,0:T(8,128)(2,1)} %bitcast.10), custom_call_target="tpu_custom_call" | custom-call | tf_op jit(solution)/shard_map/decode_bulk/pallas_call | solution.py:352
  164.7 0.0 all-to-all-done
  164.7 0.0 copy-start
  164.7 1.6 copy-done
  166.3 5.9 %decode_bulk.2 = (bf16[44,16,2048]{2,1,0:T(8,128)(2,1)}, f32[16,44]{1,0:T(8,128)}, bf16[16,2048]{1,0:T(8,128)(2,1)}) custom-call(bf16[16,2,384,128]{3,2,1,0:T(8,128)(2,1)} %bitcast.9), custom_call_target="tpu_custom_call" | custom-call | tf_op jit(solution)/shard_map/decode_bulk/pallas_call | solution.py:352
  172.2 13.8 %all_gather.3 = bf16[64,2048]{1,0:T(8,128)(2,1)S(1)} all-gather(bf16[16,2048]{1,0:T(8,128)(2,1)} %get-tuple-element.56), channel_id=1, replica_groups=mesh['ep'=4,'y'=4,'x'=4,'core'=2] {'ep'}, dimensions={0}, use_global_device_ids=true | all-gather | bytes 327680 | tf_op jit(solution)/shard_map/all_gather | solution.py:404
  186.1 0.7 copy.13
Async XLA Ops:
  60.6 104.1 %all-to-all-start = ((bf16[32,384,128]{2,1,0:T(8,128)(2,1)}), bf16[32,384,128]{2,1,0:T(8,128)(2,1)S(1)}, u32[]{:S(2)}, u32[]{:S(2)}) async-start(bf16[32,384,128]{2,1,0:T(8,128)(2,1)} %encode_bulk.2.refs_0_), calls=%async_computation | async-start | bytes 6291456 | tf_op jit(solution)/shard_map/all_to_all | solution.py:395
  67.6 3.7 %collective-permute-start = (bf16[16,368,128]{2,1,0:T(8,128)(2,1)}, bf16[16,368,128]{2,1,0:T(8,128)(2,1)}, u32[]{:S(2)}, u32[]{:S(2)}) collective-permute-start(bf16[16,368,128]{2,1,0:T(8,128)(2,1)} %get-tuple-element.33), channel_id=1, source_target_pairs={{0,1},{1,0},{2,3},{3,2},{4,5},{5,4},{6,7},{7,6},{8,9},{9,8},{10,11... | collective-permute-start | bytes 4521992 | tf_op jit(solution)/shard_map/ppermute | solution.py:397
  74.8 35.3 %collective-permute-start.1 = (bf16[2,368,128]{2,1,0:T(8,128)(2,1)}, bf16[2,368,128]{2,1,0:T(8,128)(2,1)S(1)}, u32[]{:S(2)}, u32[]{:S(2)}) collective-permute-start(bf16[2,368,128]{2,1,0:T(8,128)(2,1)} %get-tuple-element.35), channel_id=1, source_target_pairs={{0,2},{1,3},{2,4},{3,5},{4,6},{5,7},{6,0},{7,1},{8,10},{9,11},{10,... | collective-permute-start | bytes 565256 | tf_op jit(solution)/shard_map/ppermute | solution.py:383
  75.4 34.8 %collective-permute-start.2 = (bf16[2,368,128]{2,1,0:T(8,128)(2,1)}, bf16[2,368,128]{2,1,0:T(8,128)(2,1)S(1)}, u32[]{:S(2)}, u32[]{:S(2)}) collective-permute-start(bf16[2,368,128]{2,1,0:T(8,128)(2,1)} %get-tuple-element.36), channel_id=1, source_target_pairs={{0,6},{1,7},{2,0},{3,1},{4,2},{5,3},{6,4},{7,5},{8,14},{9,15},{10,... | collective-permute-start | bytes 565256 | tf_op jit(solution)/shard_map/ppermute | solution.py:383
  76.9 38.5 %collective-permute-start.3 = (bf16[2,368,128]{2,1,0:T(8,128)(2,1)}, bf16[2,368,128]{2,1,0:T(8,128)(2,1)}, u32[]{:S(2)}, u32[]{:S(2)}) collective-permute-start(bf16[2,368,128]{2,1,0:T(8,128)(2,1)} %get-tuple-element.37), channel_id=1, source_target_pairs={{0,8},{1,9},{2,10},{3,11},{4,12},{5,13},{6,14},{7,15},{8,16},{9,17... | collective-permute-start | bytes 565256 | tf_op jit(solution)/shard_map/ppermute | solution.py:383
  78.4 37.0 %collective-permute-start.4 = (bf16[2,368,128]{2,1,0:T(8,128)(2,1)}, bf16[2,368,128]{2,1,0:T(8,128)(2,1)}, u32[]{:S(2)}, u32[]{:S(2)}) collective-permute-start(bf16[2,368,128]{2,1,0:T(8,128)(2,1)} %get-tuple-element.38), channel_id=1, source_target_pairs={{0,24},{1,25},{2,26},{3,27},{4,28},{5,29},{6,30},{7,31},{8,0},{9,1... | collective-permute-start | bytes 565256 | tf_op jit(solution)/shard_map/ppermute | solution.py:383
  79.0 36.9 %collective-permute-start.5 = (bf16[2,368,128]{2,1,0:T(8,128)(2,1)}, bf16[2,368,128]{2,1,0:T(8,128)(2,1)}, u32[]{:S(2)}, u32[]{:S(2)}) collective-permute-start(bf16[2,368,128]{2,1,0:T(8,128)(2,1)} %get-tuple-element.39), channel_id=1, source_target_pairs={{0,10},{1,11},{2,12},{3,13},{4,14},{5,15},{6,8},{7,9},{8,18},{9,19... | collective-permute-start | bytes 565256 | tf_op jit(solution)/shard_map/ppermute | solution.py:383
  110.2 42.2 %copy-start.1 = (bf16[2,368,128]{2,1,0:T(8,128)(2,1)}, bf16[2,368,128]{2,1,0:T(8,128)(2,1)S(1)}, u32[]{:S(2)}) copy-start(bf16[2,368,128]{2,1,0:T(8,128)(2,1)S(1)} %collective-permute-done.1.refs_1_) | copy-start | bytes 565252
  110.2 11.1 %collective-permute-start.6 = (bf16[2,368,128]{2,1,0:T(8,128)(2,1)}, bf16[2,368,128]{2,1,0:T(8,128)(2,1)}, u32[]{:S(2)}, u32[]{:S(2)}) collective-permute-start(bf16[2,368,128]{2,1,0:T(8,128)(2,1)} %get-tuple-element.40), channel_id=1, source_target_pairs={{0,30},{1,31},{2,24},{3,25},{4,26},{5,27},{6,28},{7,29},{8,6},{9,7... | collective-permute-start | bytes 565256 | tf_op jit(solution)/shard_map/ppermute | solution.py:383
  110.2 42.2 %copy-start.2 = (bf16[2,368,128]{2,1,0:T(8,128)(2,1)}, bf16[2,368,128]{2,1,0:T(8,128)(2,1)S(1)}, u32[]{:S(2)}) copy-start(bf16[2,368,128]{2,1,0:T(8,128)(2,1)S(1)} %collective-permute-done.2.refs_2_) | copy-start | bytes 565252
  110.2 11.9 %collective-permute-start.7 = (bf16[2,368,128]{2,1,0:T(8,128)(2,1)}, bf16[2,368,128]{2,1,0:T(8,128)(2,1)}, u32[]{:S(2)}, u32[]{:S(2)}) collective-permute-start(bf16[2,368,128]{2,1,0:T(8,128)(2,1)} %get-tuple-element.41), channel_id=1, source_target_pairs={{0,26},{1,27},{2,28},{3,29},{4,30},{5,31},{6,24},{7,25},{8,2},{9,3... | collective-permute-start | bytes 565256 | tf_op jit(solution)/shard_map/ppermute | solution.py:383
  115.5 20.7 %collective-permute-start.8 = (bf16[2,368,128]{2,1,0:T(8,128)(2,1)}, bf16[2,368,128]{2,1,0:T(8,128)(2,1)}, u32[]{:S(2)}, u32[]{:S(2)}) collective-permute-start(bf16[2,368,128]{2,1,0:T(8,128)(2,1)} %get-tuple-element.42), channel_id=1, source_target_pairs={{0,14},{1,15},{2,8},{3,9},{4,10},{5,11},{6,12},{7,13},{8,22},{9,23... | collective-permute-start | bytes 565256 | tf_op jit(solution)/shard_map/ppermute | solution.py:383
  115.5 20.7 %collective-permute-start.9 = (bf16[2,368,128]{2,1,0:T(8,128)(2,1)}, bf16[2,368,128]{2,1,0:T(8,128)(2,1)}, u32[]{:S(2)}, u32[]{:S(2)}) collective-permute-start(bf16[2,368,128]{2,1,0:T(8,128)(2,1)} %get-tuple-element.43), channel_id=1, source_target_pairs={{0,4},{1,5},{2,6},{3,7},{4,0},{5,1},{6,2},{7,3},{8,12},{9,13},{10,... | collective-permute-start | bytes 565256 | tf_op jit(solution)/shard_map/ppermute | solution.py:383
  115.9 24.8 %collective-permute-start.10 = (bf16[2,368,128]{2,1,0:T(8,128)(2,1)}, bf16[2,368,128]{2,1,0:T(8,128)(2,1)}, u32[]{:S(2)}, u32[]{:S(2)}) collective-permute-start(bf16[2,368,128]{2,1,0:T(8,128)(2,1)} %get-tuple-element.44), channel_id=1, source_target_pairs={{0,16},{1,17},{2,18},{3,19},{4,20},{5,21},{6,22},{7,23},{8,24},{9,... | collective-permute-start | bytes 565256 | tf_op jit(solution)/shard_map/ppermute | solution.py:383
  121.3 19.4 %collective-permute-start.11 = (bf16[2,368,128]{2,1,0:T(8,128)(2,1)}, bf16[2,368,128]{2,1,0:T(8,128)(2,1)}, u32[]{:S(2)}, u32[]{:S(2)}) collective-permute-start(bf16[2,368,128]{2,1,0:T(8,128)(2,1)} %get-tuple-element.45), channel_id=1, source_target_pairs={{0,12},{1,13},{2,14},{3,15},{4,8},{5,9},{6,10},{7,11},{8,20},{9,21... | collective-permute-start | bytes 565256 | tf_op jit(solution)/shard_map/ppermute | solution.py:383
  122.1 18.6 %collective-permute-start.12 = (bf16[2,368,128]{2,1,0:T(8,128)(2,1)}, bf16[2,368,128]{2,1,0:T(8,128)(2,1)}, u32[]{:S(2)}, u32[]{:S(2)}) collective-permute-start(bf16[2,368,128]{2,1,0:T(8,128)(2,1)} %get-tuple-element.46), channel_id=1, source_target_pairs={{0,28},{1,29},{2,30},{3,31},{4,24},{5,25},{6,26},{7,27},{8,4},{9,5... | collective-permute-start | bytes 565256 | tf_op jit(solution)/shard_map/ppermute | solution.py:383
  136.2 12.4 %collective-permute-start.13 = (bf16[2,368,128]{2,1,0:T(8,128)(2,1)}, bf16[2,368,128]{2,1,0:T(8,128)(2,1)}, u32[]{:S(2)}, u32[]{:S(2)}) collective-permute-start(bf16[2,368,128]{2,1,0:T(8,128)(2,1)} %get-tuple-element.47), channel_id=1, source_target_pairs={{0,18},{1,19},{2,20},{3,21},{4,22},{5,23},{6,16},{7,17},{8,26},{9,... | collective-permute-start | bytes 565256 | tf_op jit(solution)/shard_map/ppermute | solution.py:383
  136.2 16.2 %collective-permute-start.14 = (bf16[2,368,128]{2,1,0:T(8,128)(2,1)}, bf16[2,368,128]{2,1,0:T(8,128)(2,1)}, u32[]{:S(2)}, u32[]{:S(2)}) collective-permute-start(bf16[2,368,128]{2,1,0:T(8,128)(2,1)} %get-tuple-element.48), channel_id=1, source_target_pairs={{0,22},{1,23},{2,16},{3,17},{4,18},{5,19},{6,20},{7,21},{8,30},{9,... | collective-permute-start | bytes 565256 | tf_op jit(solution)/shard_map/ppermute | solution.py:383
  140.6 11.7 %collective-permute-start.15 = (bf16[2,368,128]{2,1,0:T(8,128)(2,1)}, bf16[2,368,128]{2,1,0:T(8,128)(2,1)}, u32[]{:S(2)}, u32[]{:S(2)}) collective-permute-start(bf16[2,368,128]{2,1,0:T(8,128)(2,1)} %get-tuple-element.49), channel_id=1, source_target_pairs={{0,20},{1,21},{2,22},{3,23},{4,16},{5,17},{6,18},{7,19},{8,28},{9,... | collective-permute-start | bytes 565256 | tf_op jit(solution)/shard_map/ppermute | solution.py:383
  164.7 1.6 copy-start
where the time goes:
time: 187 us
  waiting for transfers between devices  57.3 us (31%)
  blocking collectives  56.7 us (30%)
  Pallas kernels  38.7 us (21%)
  starting transfers between devices  31 us (17%)
  local copies, waits for them, and re-layouts  2.34 us (1%)
    ppermute x15, waiting for transfers between devices, moved(): return lax.ppermute(value, PLANE, pairs)  53.7 us
    all_to_all x1, blocking collectives, body(): arrived_second = lax.all_to_all(second, PLANE, 0, 0, tiled=True)  42.9 us
    ppermute x15, starting transfers between devices, moved(): return lax.ppermute(value, PLANE, pairs)  23.7 us
    pallas_call x3, Pallas kernels, decode(): pl.pallas_call(functools.partial(decode_kernel, share, depth, head, route...  18.2 us
    all_gather x1, blocking collectives, body(): router = lax.all_gather(router, 'ep', axis=0, tiled=True)  13.8 us
    pallas_call x2, Pallas kernels, encode_bulk(): pl.pallas_call(behind(len(ahead), functools.partial(encode_bulk_kernel, r...  11.2 us
    all_to_all x1, starting transfers between devices, body(): arrived_first = lax.all_to_all(first, PLANE, 0, 0, tiled=True)  7.03 us
    pallas_call x1, Pallas kernels, encode_head(): pl.pallas_call(behind(len(ahead), functools.partial(encode_head_kernel, p...  5.87 us
  transfers between devices with their start and end apart: 17, of which 7 were waited for; matrix products, arithmetic and copies ran while one was open for 0% of the time, Pallas kernels for 8%

commit v1 on v0

v1 whole, which is shorter than its diff:
```python
import functools

import jax
import jax.numpy as jnp
from jax import lax
from jax.experimental import pallas as pl
from jax.experimental.pallas import tpu as pltpu
from jax.sharding import Mesh, PartitionSpec as P


POWER = 17
REACH = 180.0
FLOOR = 1e-37
LANES = 128
HALF = LANES // 2
STEP = 4
SIDE = 4
CHIPS = SIDE * SIDE
PLANE = ("y", "x", "core")
TURNS = (1, 3, 2)


def anywhere(count):
    return [pl.BlockSpec(memory_space=pl.ANY)] * count


def rows_at(start, size, unit):
    return pl.ds(pl.multiple_of(start, unit), size)


def landed(ref, sem):
    pltpu.make_async_copy(ref, ref, sem).wait()


def chip_at(dx, dy):
    y, x = lax.axis_index("y"), lax.axis_index("x")
    return lax.rem(y + dy, SIDE) * SIDE + lax.rem(x + dx, SIDE)


def behind(ahead, kernel):
    return lambda *refs: kernel(*refs[ahead:])


def encode_tiles(x, xin, stage, pay, sums, notes, sem_in, peers, tiles, after):
    depth, experts, _, _ = xin.shape
    half = experts // 2
    share = tiles * LANES // peers
    odd = lax.axis_index("core")

    def fetch(i):
        slot = lax.rem(i, depth)
        at = rows_at(i * LANES, LANES, LANES)
        pltpu.make_async_copy(x.at[:, :, at], xin.at[slot], sem_in.at[slot]).start()

    def first(i, carry):
        fetch(i)
        return carry

    lax.fori_loop(0, depth, first, 0)

    def tile_of(i, carry):
        slot = lax.rem(i, depth)
        landed(xin.at[slot], sem_in.at[slot])
        at = rows_at(i * LANES, LANES, LANES)
        for e in range(half):
            a, b = xin[slot, e + half * odd], xin[slot, e + half * (1 - odd)]
            sa = jnp.sum(a * a, 0, keepdims=True)
            sb = jnp.sum(b * b, 0, keepdims=True)
            sums[pl.ds(e, 1), at] = sa
            sums[pl.ds(e + half, 1), at] = sb
            a = a * (REACH * lax.rsqrt(jnp.maximum(sa, FLOOR)))
            b = b * (REACH * lax.rsqrt(jnp.maximum(sb, FLOOR)))
            v = jnp.concatenate([a, b], 0)
            v2 = v * v
            v4 = v2 * v2
            v8 = v4 * v4
            y = v8 * v8 * v
            stage[pl.ds(e, LANES, stride=half), :] = y.T
        pay[rows_at(i * LANES * half, LANES * half, LANES * half), :] = stage[...].astype(jnp.bfloat16)

        @pl.when(i + depth < tiles)
        def _():
            fetch(i + depth)

        after(i)
        return carry

    lax.fori_loop(0, tiles, tile_of, 0)
    total = sums[...]
    total = jnp.where(odd == 1, jnp.concatenate([total[half:], total[:half]], 0), total)
    high = total.astype(jnp.bfloat16).astype(jnp.float32)
    low = total - high
    gap = jnp.zeros((experts, HALF - share), jnp.float32)
    for d in range(peers):
        piece = slice(d * share, (d + 1) * share)
        notes[d] = jnp.concatenate([high[:, piece], gap, low[:, piece], gap], 1).astype(jnp.bfloat16)


def encode_scratch(peers, experts, rows, columns, depth):
    return [
        pltpu.VMEM((depth, experts, rows, LANES), jnp.float32),
        pltpu.VMEM((LANES * experts // 2, LANES), jnp.float32),
        pltpu.VMEM((columns * experts // 2, LANES), jnp.bfloat16),
        pltpu.VMEM((experts, columns), jnp.float32),
        pltpu.VMEM((peers, experts, LANES), jnp.bfloat16),
        pltpu.SemaphoreType.DMA((depth,)),
        pltpu.SemaphoreType.DMA,
        pltpu.SemaphoreType.DMA,
    ]


def encode_bulk_kernel(routed, peers, tiles, *refs):
    x, out = refs[0], refs[1 + 2 * routed]
    xin, stage, pay, sums, notes, sem_in, sem_pay, sem_note = refs[2 + 2 * routed : 10 + 2 * routed]
    experts = xin.shape[1]
    half = experts // 2
    share = tiles * LANES // peers
    block = share * half

    if routed:
        weight, gain = refs[1:3]
        router, sem_router = refs[10 + 2 * routed :]
        part = weight[...] * gain[...]
        part = jnp.where(lax.axis_index("core") == 1, jnp.concatenate([part[half:], part[:half]], 0), part)
        part = jnp.concatenate([part[:half], part[half:]], 1)
        part = jnp.concatenate([part, jnp.zeros_like(part)], 0).astype(jnp.bfloat16)
        for d in range(peers):
            router[d] = part
        pltpu.make_async_copy(router, out.at[:, pl.ds(block + experts, experts), :], sem_router).start()

    def after(tile):
        def send(d, inner):
            pltpu.make_async_copy(
                pay.at[rows_at(d * block, block, 16), :], out.at[d, pl.ds(0, block), :], sem_pay
            ).start()
            return inner

        lax.fori_loop(tile * LANES // share, (tile + 1) * LANES // share, send, 0)

    encode_tiles(x, xin, stage, pay, sums, notes, sem_in, peers, tiles, after)
    pltpu.make_async_copy(notes, out.at[:, pl.ds(block, experts), :], sem_note).start()
    landed(pay, sem_pay)
    landed(notes, sem_note)
    if routed:
        landed(router, sem_router)


def encode_bulk(x, small, ahead, peers, depth=8):
    experts, rows, columns = x.shape
    routed = len(small) // 2
    height = columns // peers * experts // 2 + experts * (1 + routed)
    return pl.pallas_call(
        behind(len(ahead), functools.partial(encode_bulk_kernel, routed, peers, columns // LANES)),
        in_specs=anywhere(len(ahead) + 1) + [pl.BlockSpec(memory_space=pltpu.VMEM)] * len(small),
        out_specs=pl.BlockSpec(memory_space=pl.ANY),
        out_shape=jax.ShapeDtypeStruct((peers, height, LANES), jnp.bfloat16),
        scratch_shapes=encode_scratch(peers, experts, rows, columns, depth)
        + [pltpu.VMEM((peers, experts, LANES), jnp.bfloat16), pltpu.SemaphoreType.DMA] * routed,
        name="encode_bulk",
    )(*ahead, x, *small)


def encode_head_kernel(peers, tiles, cut, x, *refs):
    by_x, by_y, scratch = refs[:SIDE], refs[SIDE : 2 * SIDE], refs[2 * SIDE :]
    xin, stage, pay, sums, notes, sem_in, sem_pay, sem_note = scratch
    experts = xin.shape[1]
    block = tiles * LANES // peers * experts // 2
    encode_tiles(x, xin, stage, pay, sums, notes, sem_in, peers, tiles, lambda tile: None)
    for dx in range(SIDE):
        for dy in range(SIDE):
            for core in range(2):
                d = 2 * chip_at(dx, dy) + core
                for out, start, size in (
                    (by_x[dx].at[core, dy], 0, cut),
                    (by_y[dy].at[core, dx, pl.ds(0, block - cut)], cut, block - cut),
                ):
                    pltpu.make_async_copy(pay.at[rows_at(d * block + start, size, 16), :], out, sem_pay).start()
                out = by_y[dy].at[core, dx, pl.ds(block - cut, experts)]
                pltpu.make_async_copy(notes.at[d], out, sem_note).start()
    landed(pay, sem_pay)
    landed(notes, sem_note)


def encode_head(x, cut, ahead, peers, depth=8):
    experts, rows, columns = x.shape
    height = columns // peers * experts // 2 + experts
    return pl.pallas_call(
        behind(len(ahead), functools.partial(encode_head_kernel, peers, columns // LANES, cut)),
        in_specs=anywhere(len(ahead) + 1),
        out_specs=anywhere(2 * SIDE),
        out_shape=[
            jax.ShapeDtypeStruct((2, SIDE, size, LANES), jnp.bfloat16)
            for size in (cut, height - cut)
            for _ in range(SIDE)
        ],
        scratch_shapes=encode_scratch(peers, experts, rows, columns, depth),
        name="encode_head",
    )(*ahead, x)


def sift_kernel(*refs):
    ins, give, (held_x, held_y, sem_in, sem_out) = refs[: 2 * SIDE], refs[2 * SIDE], refs[2 * SIDE + 1 :]
    other = 1 - lax.axis_index("core")
    cut, rest = held_x.shape[2], held_y.shape[2]
    for g, held in enumerate((held_x, held_y)):
        for i in range(SIDE):
            pltpu.make_async_copy(ins[SIDE * g + i].at[other], held.at[i], sem_in.at[g]).start()
    landed(held_x, sem_in.at[0])
    for i in range(SIDE):
        pltpu.make_async_copy(held_x.at[i], give.at[i, :, pl.ds(0, cut)], sem_out.at[0]).start()
    landed(held_y, sem_in.at[1])
    for i in range(SIDE):
        pltpu.make_async_copy(held_y.at[i], give.at[i, :, pl.ds(cut, rest)], sem_out.at[1]).start()
    landed(held_x, sem_out.at[0])
    landed(held_y, sem_out.at[1])


def sifted(arrays):
    cut, rest = arrays[0].shape[2], arrays[SIDE].shape[2]
    return pl.pallas_call(
        sift_kernel,
        in_specs=anywhere(2 * SIDE),
        out_specs=pl.BlockSpec(memory_space=pl.ANY),
        out_shape=jax.ShapeDtypeStruct((SIDE, SIDE, cut + rest, LANES), jnp.bfloat16),
        scratch_shapes=[pltpu.VMEM((SIDE, SIDE, size, LANES), jnp.bfloat16) for size in (cut, rest)]
        + [pltpu.SemaphoreType.DMA((2,)), pltpu.SemaphoreType.DMA((2,))],
        name="sifted",
    )(*arrays)


def cross_kernel(got, *refs):
    ins, outs, (held_x, held_y, sem_in, sem_out) = refs[:8], refs[8:16], refs[16:]
    core = lax.axis_index("core")
    start = 0
    for g, held in enumerate((held_x, held_y)):
        size = held.shape[3]
        for i in range(SIDE):
            pltpu.make_async_copy(ins[SIDE * g + i].at[core], held.at[0, i], sem_in.at[g]).start()
            pltpu.make_async_copy(got.at[i, :, pl.ds(start, size)], held.at[1, i], sem_in.at[g]).start()
        start += size
    for g, held in enumerate((held_x, held_y)):
        landed(held, sem_in.at[g])
        for j in range(SIDE):
            pltpu.make_async_copy(held.at[:, :, j], outs[SIDE * g + j], sem_out.at[g]).start()
    for g, held in enumerate((held_x, held_y)):
        landed(held, sem_out.at[g])


def crossed(got, arrays):
    shapes = [a.shape for a in arrays]
    return pl.pallas_call(
        cross_kernel,
        in_specs=anywhere(1 + 2 * SIDE),
        out_specs=anywhere(2 * SIDE),
        out_shape=[jax.ShapeDtypeStruct(shape, jnp.bfloat16) for shape in shapes],
        scratch_shapes=[pltpu.VMEM((2, SIDE, *shapes[k][1:]), jnp.bfloat16) for k in (0, SIDE)]
        + [pltpu.SemaphoreType.DMA((2,)), pltpu.SemaphoreType.DMA((2,))],
        name="crossed",
    )(got, *arrays)


def two_cores(a, b):
    left = lax.broadcasted_iota(jnp.int32, a.shape, 1) < HALF
    return jnp.concatenate([jnp.where(left, a, b), pltpu.roll(jnp.where(left, b, a), HALF, 1)], 0)


def plain(code):
    y = code.astype(jnp.float32)
    size = jnp.maximum(jnp.abs(y), 1.2e-38)
    return y * jnp.exp2(jnp.log2(size) * (1.0 / POWER - 1.0))


COPIES = 3


def spread_picks(picks):
    row = lax.broadcasted_iota(jnp.int32, (LANES, LANES), 0)
    right = jnp.where(lax.broadcasted_iota(jnp.int32, (LANES, LANES), 1) < HALF, 0, 1)
    peer = jnp.where(row < COPIES * 2 * CHIPS, lax.rem(row, 2 * CHIPS), -1)
    for q in range(CHIPS):
        picks[:, q * LANES : (q + 1) * LANES] = jnp.where(peer == 2 * q + right, 1.0, 0.0).astype(jnp.bfloat16)


def factors_from(notes, scale_out, factors, turned, ready_factors):
    experts, share = scale_out.shape
    part = notes[...].astype(jnp.float32).reshape(2 * CHIPS, experts, LANES)
    part = part + pltpu.roll(part, HALF, 2)
    scale = jnp.sqrt(jnp.sum(part, 0))
    scale_out[...] = scale[:, :share]
    part = jnp.sqrt(jnp.maximum(part, FLOOR)) * (1.0 / (REACH * scale))[None]
    factors[...] = part.reshape(2 * CHIPS * experts, LANES)
    tall = ready_factors.shape[0] // experts
    for e in range(experts):
        value = factors[pl.ds(e, 2 * CHIPS, stride=experts), :]
        pieces = []
        for _ in range(COPIES):
            pieces.append(value.astype(jnp.bfloat16).astype(jnp.float32))
            value = value - pieces[-1]
        pieces.append(jnp.zeros((LANES - COPIES * 2 * CHIPS, LANES), jnp.float32))
        turned[pl.ds(e, tall, stride=experts), :] = jnp.concatenate(pieces, 0).T[:tall]
    ready_factors[...] = turned[...].astype(jnp.bfloat16)


def decode_step(s, ready_out, ready_factors, picks, ready, sem_out, load, place):
    outs, _, experts, _ = ready.shape
    half = experts // 2
    out_slot = lax.rem(s, outs)

    @pl.when(s >= outs)
    def _():
        landed(ready.at[out_slot], sem_out.at[out_slot])

    known = ready_factors[rows_at(s * STEP * experts, STEP * experts, STEP * experts), :]
    for q in range(CHIPS):
        if q % 2 == 0:
            wide = picks[:, q * LANES : (q + 2) * LANES]
            factor = jnp.dot(known, wide, preferred_element_type=jnp.float32)
        mine = factor[:, q % 2 * LANES : (q % 2 + 1) * LANES]
        for p in range(STEP // 2):
            a2, b2 = (plain(load(q, which, p)) for which in range(2))
            for h in range(2):
                j = 2 * p + h
                value = two_cores(a2[half * h : half * (h + 1)], b2[half * h : half * (h + 1)])
                value = value * mine[experts * j : experts * (j + 1)]
                ready[out_slot, j, :, rows_at(place(q) * LANES, LANES, LANES)] = value.astype(jnp.bfloat16)
    pltpu.make_async_copy(ready.at[out_slot], ready_out.at[pl.ds(s * STEP, STEP)], sem_out.at[out_slot]).start()


def decode_scratch(experts, share, rows, outs):
    tall = -(-share // 8) * 8
    return [
        pltpu.VMEM((2 * CHIPS * experts, LANES), jnp.float32),
        pltpu.VMEM((tall * experts, LANES), jnp.float32),
        pltpu.VMEM((tall * experts, LANES), jnp.bfloat16),
        pltpu.VMEM((LANES, CHIPS * LANES), jnp.bfloat16),
        pltpu.VMEM((outs, STEP, experts, rows * 2 * CHIPS), jnp.bfloat16),
        pltpu.SemaphoreType.DMA((outs,)),
    ]


def decoded_shapes(experts, share, rows):
    return [
        jax.ShapeDtypeStruct((share, experts, rows * 2 * CHIPS), jnp.bfloat16),
        jax.ShapeDtypeStruct((experts, share), jnp.float32),
    ]


def decode_bulk_kernel(depth, source, ready_out, scale_out, router, pay, notes, sem_in, sem_note, *scratch):
    factors, turned, ready_factors, picks, ready, sem_out = scratch
    experts, share = scale_out.shape
    half = experts // 2
    height = STEP * half
    steps = share // STEP

    def fetch(i):
        slot = lax.rem(i, depth)
        rows = rows_at(i * height, height, height)
        pltpu.make_async_copy(source.at[:, :, rows, :], pay.at[slot], sem_in.at[slot]).start()

    for k in range(2):
        rows = pl.ds(share * half + k * experts, experts)
        pltpu.make_async_copy(source.at[:, :, rows, :], notes.at[k], sem_note.at[k]).start()

    def first(i, carry):
        fetch(i)
        return carry

    lax.fori_loop(0, depth, first, 0)
    spread_picks(picks)
    landed(notes.at[1], sem_note.at[1])
    for q in range(CHIPS):
        a, b = (notes[1, q, c].astype(jnp.float32)[:half] for c in range(2))
        router[:, q * LANES : (q + 1) * LANES] = two_cores(a, b).astype(jnp.bfloat16)
    landed(notes.at[0], sem_note.at[0])
    factors_from(notes.at[0], scale_out, factors, turned, ready_factors)

    def step_of(s, carry):
        slot = lax.rem(s, depth)
        landed(pay.at[slot], sem_in.at[slot])

        def load(q, which, p):
            return pay[slot, q, which, 2 * half * p : 2 * half * (p + 1), :]

        decode_step(s, ready_out, ready_factors, picks, ready, sem_out, load, lambda q: q)

        @pl.when(s + depth < steps)
        def _():
            fetch(s + depth)

        return carry

    lax.fori_loop(0, steps, step_of, 0)
    for slot in range(ready.shape[0]):
        landed(ready.at[slot], sem_out.at[slot])


def decode_bulk(source, experts, share, rows, depth=8, outs=6):
    vmem = pl.BlockSpec(memory_space=pltpu.VMEM)
    return pl.pallas_call(
        functools.partial(decode_bulk_kernel, depth),
        in_specs=anywhere(1),
        out_specs=anywhere(1) + [vmem] * 2,
        out_shape=decoded_shapes(experts, share, rows)
        + [jax.ShapeDtypeStruct((experts, rows * 2 * CHIPS), jnp.bfloat16)],
        scratch_shapes=[
            pltpu.VMEM((depth, CHIPS, 2, STEP * experts // 2, LANES), jnp.bfloat16),
            pltpu.VMEM((2, CHIPS, 2, experts, LANES), jnp.bfloat16),
            pltpu.SemaphoreType.DMA((depth,)),
            pltpu.SemaphoreType.DMA((2,)),
        ]
        + decode_scratch(experts, share, rows, outs),
        name="decode_bulk",
    )(source)


def decode_head_kernel(*refs):
    by_x, by_y, refs = refs[:SIDE], refs[SIDE : 2 * SIDE], refs[2 * SIDE :]
    ready_out, scale_out, *refs = refs
    held_x, held_y, notes, sem_in, sem_note, factors, turned, ready_factors, picks, ready, sem_out = refs
    experts, share = scale_out.shape
    half = experts // 2
    height = STEP * half
    steps = share // STEP
    turn = held_x.shape[3] // height
    core = lax.axis_index("core")
    even = (core, 1 - core)

    for i in range(SIDE):
        rows = pl.ds((steps - turn) * height, experts)
        pltpu.make_async_copy(by_y[i].at[:, :, rows], held_y.at[i, :, :, rows], sem_note).start()
    for s in range(steps):
        arrays, held, at = (by_x, held_x, s) if s < turn else (by_y, held_y, s - turn)
        rows = pl.ds(at * height, height)
        for i in range(SIDE):
            pltpu.make_async_copy(arrays[i].at[:, :, rows], held.at[i, :, :, rows], sem_in.at[s]).start()
    spread_picks(picks)
    landed(notes, sem_note)
    for dx in range(SIDE):
        for dy in range(SIDE):
            for which in range(2):
                rows = pl.ds((steps - turn) * height, experts)
                notes[SIDE * dx + dy, which] = held_y[dx, even[which], dy, rows, :]
    factors_from(notes, scale_out, factors, turned, ready_factors)

    def place(q):
        return chip_at(SIDE - q // SIDE, SIDE - q % SIDE)

    def step_with(held, first):
        def step_of(s, carry):
            landed(held.at[:, :, :, pl.ds(0, height)], sem_in.at[s])

            def load(q, which, p):
                i, j = (q % SIDE, q // SIDE) if first == 0 else (q // SIDE, q % SIDE)
                rows = rows_at((s - first) * height + 2 * half * p, 2 * half, 2 * half)
                return held[i, even[which], j, rows, :]

            decode_step(s, ready_out, ready_factors, picks, ready, sem_out, load, place)
            return carry

        return step_of

    lax.fori_loop(0, turn, step_with(held_x, 0), 0)
    lax.fori_loop(turn, steps, step_with(held_y, turn), 0)
    for slot in range(ready.shape[0]):
        landed(ready.at[slot], sem_out.at[slot])


def decode_head(parts, experts, share, rows, outs=6):
    vmem = pl.BlockSpec(memory_space=pltpu.VMEM)
    return pl.pallas_call(
        decode_head_kernel,
        in_specs=anywhere(len(parts)),
        out_specs=anywhere(1) + [vmem],
        out_shape=decoded_shapes(experts, share, rows),
        scratch_shapes=[pltpu.VMEM((SIDE, *parts[k].shape), jnp.bfloat16) for k in (0, SIDE)]
        + [
            pltpu.VMEM((CHIPS, 2, experts, LANES), jnp.bfloat16),
            pltpu.SemaphoreType.DMA((share // STEP,)),
            pltpu.SemaphoreType.DMA,
        ]
        + decode_scratch(experts, share, rows, outs),
        name="decode_head",
    )(*parts)


def join_kernel(*refs):
    parts, out = refs[:-1], refs[-1]
    count = len(parts)
    for k, part in enumerate(parts):
        plane = lax.rem(lax.axis_index("ep") + count - k, count)
        out[rows_at(plane * part.shape[0], part.shape[0], part.shape[0]), :] = part[...]


def joined(parts):
    rows, columns = parts[0].shape
    vmem = pl.BlockSpec(memory_space=pltpu.VMEM)
    return pl.pallas_call(
        join_kernel,
        in_specs=[vmem] * len(parts),
        out_specs=vmem,
        out_shape=jax.ShapeDtypeStruct((len(parts) * rows, columns), parts[0].dtype),
        name="joined",
    )(*parts)


def moved(value, axis, shift):
    return lax.ppermute(value, axis, [(k, (k + shift) % SIDE) for k in range(SIDE)])


def body(train_gate, train_up, train_down, router_weight, router_gain):
    peers = lax.axis_size(PLANE)
    experts, rows, columns = train_gate.shape
    share = columns // peers

    cut = STEP * experts // 2 * 6

    def phase(parts, axes):
        parts = list(parts)
        for shift in TURNS:
            for g, axis in enumerate(axes):
                parts[SIDE * g + shift] = moved(parts[SIDE * g + shift], axis, shift)
        return parts

    def halfway(parts):
        give = sifted(parts)
        got = lax.ppermute(give, "core", ((0, 1), (1, 0)))
        return crossed(got, parts)

    gate = encode_head(train_gate, cut, (), peers)
    first = encode_bulk(train_up, (router_weight.T, router_gain[None]), (gate[0],), peers)
    gate = phase(gate, ("x", "y"))
    arrived = lax.all_to_all(first, PLANE, 0, 0, tiled=True)
    down = encode_head(jnp.swapaxes(train_down, 1, 2), cut, (first,), peers)
    down = phase(down, ("x", "y"))
    gate = phase(halfway(gate), ("y", "x"))
    arrived = arrived.reshape(CHIPS, 2, *arrived.shape[1:])
    up, scale_up, router = decode_bulk(arrived, experts, share, rows)
    down = phase(halfway(down), ("y", "x"))
    planes = [router]
    for k in range(1, lax.axis_size("ep")):
        planes.append(moved(router, "ep", k))
    router = joined(planes)
    gate, scale_gate = decode_head(gate, experts, share, rows)
    down, scale_down = decode_head(down, experts, share, rows)
    return (
        jnp.transpose(gate, (1, 2, 0)),
        jnp.transpose(up, (1, 2, 0)),
        jnp.transpose(down, (1, 0, 2)),
        scale_gate,
        scale_up,
        scale_down,
        router.T,
    )


def solution(mesh):
    fine = Mesh(mesh.devices.reshape(mesh.devices.shape[0], SIDE, SIDE, 2), ("ep",) + PLANE)


    return jax.shard_map(
        body,
        mesh=fine,
        in_specs=(
            P("ep", PLANE, None),
            P("ep", PLANE, None),
            P("ep", None, PLANE),
            P(PLANE, "ep"),
            P(PLANE),
        ),
        out_specs=(
            P("ep", None, PLANE),
            P("ep", None, PLANE),
            P("ep", PLANE, None),
            P("ep", PLANE),
            P("ep", PLANE),
            P("ep", PLANE),
            P(),
        ),
        check_vma=False,
    )
```

time: 187 us -> 175 us (0.936)
  the two profiles are of different devices: /device:TPU:14 before, /device:TPU:4 now
where the time goes in v1:
time: 175 us; the launch traced here: 174 us
  waiting for transfers between devices  75.7 us (43%)
  Pallas kernels  48.8 us (28%)
  starting transfers between devices  45.3 us (26%)
  local copies, waits for them, and re-layouts  3.65 us (2%)
    ppermute x27, waiting for transfers between devices, moved(): lax.ppermute(value, axis, [(k, (k + shift) % SIDE) for k in range(SIDE)])  75.7 us
    ppermute x27, starting transfers between devices, moved(): lax.ppermute(value, axis, [(k, (k + shift) % SIDE) for k in range(SIDE)])  38.7 us
    pallas_call x2, Pallas kernels, decode_head(): pl.pallas_call(decode_head_kernel, in_specs=anywhere(len(parts)), out_spe...  12.6 us
    pallas_call x2, Pallas kernels, encode_head(): pl.pallas_call(behind(len(ahead), functools.partial(encode_head_kernel, p...  11.7 us
    all_to_all x1, starting transfers between devices, body(): arrived = lax.all_to_all(first, PLANE, 0, 0, tiled=True)  6.48 us
    pallas_call x2, Pallas kernels, crossed(): pl.pallas_call(cross_kernel, in_specs=anywhere(1 + 2 * SIDE), out_specs=a...  6.2 us
    pallas_call x1, Pallas kernels, encode_bulk(): pl.pallas_call(behind(len(ahead), functools.partial(encode_bulk_kernel, r...  6.01 us
    pallas_call x1, Pallas kernels, decode_bulk(): pl.pallas_call(functools.partial(decode_bulk_kernel, depth), in_specs=any...  5.92 us
  transfers between devices with their start and end apart: 30, of which 11 were waited for; matrix products, arithmetic and copies ran while one was open for 0% of the time, Pallas kernels for 24%

profile of v1, /device:TPU:4, one launch (start us, length us, event | category | flops | bytes accessed | tf_op | source)
XLA Modules:
  0.0 174.3 jit_solution(11070595151398193575)
XLA Ops:
  0.6 5.9 %encode_head.2 = (bf16[2,4,192,128]{3,2,1,0:T(8,128)(2,1)}, bf16[2,4,192,128]{3,2,1,0:T(8,128)(2,1)}, bf16[2,4,192,128]{3,2,1,0:T(8,128)(2,1)}, bf16[2,4,192,128...) custom-call(f32[16,64,1408]{2,1,0:T(8,128)} %refs_0_.1), custom_call_target="tpu_custom_call" | custom-call | tf_op jit(solution)/shard_map/encode_head/pallas_call | solution.py:187
  6.5 1.6 collective-permute-start.3
  8.1 2.9 %collective-permute-start.4 = (bf16[2,4,176,128]{3,2,1,0:T(8,128)(2,1)}, bf16[2,4,176,128]{3,2,1,0:T(8,128)(2,1)}, u32[]{:S(2)}, u32[]{:S(2)}) collective-permute-start(bf16[2,4,176,128]{3,2,1,0:T(8,128)(2,1)} %get-tuple-element.52), channel_id=1, source_target_pairs={{0,16},{8,24},{16,0},{24,8},{1,17},{9,25},{17,1},{25,9},{2,18},{10... | collective-permute-start | bytes 1081352 | tf_op jit(solution)/shard_map/ppermute | solution.py:507
  11.0 1.3 collective-permute-start.5
  12.4 1.2 collective-permute-start
  13.6 0.8 collective-permute-start.1
  14.4 6.0 %encode_bulk.1.refs_0_ = bf16[32,384,128]{2,1,0:T(8,128)(2,1)} custom-call(bf16[2,4,192,128]{3,2,1,0:T(8,128)(2,1)} %get-tuple-element.46.refs_0_, f32[16,64,1408]{2,1,0:T(8,128)} %refs_1_.1, f32[16,64]{1,0:T(8,128)} %bitcast.11, f32[1,64]{1,0:T(1,128)} %bitcast.12), custom_call_target="tpu_custom_call" | custom-call | tf_op jit(solution)/shard_map/encode_bulk/pallas_call | solution.py:152
  20.4 6.5 %all-to-all-start = ((bf16[32,384,128]{2,1,0:T(8,128)(2,1)}), bf16[32,384,128]{2,1,0:T(8,128)(2,1)S(1)}, u32[]{:S(2)}, u32[]{:S(2)}) async-start(bf16[32,384,128]{2,1,0:T(8,128)(2,1)} %encode_bulk.1.refs_0_), calls=%async_computation | async-start | bytes 6291456 | tf_op jit(solution)/shard_map/all_to_all | solution.py:532
  26.9 5.8 %encode_head.3 = (bf16[2,4,192,128]{3,2,1,0:T(8,128)(2,1)}, bf16[2,4,192,128]{3,2,1,0:T(8,128)(2,1)}, bf16[2,4,192,128]{3,2,1,0:T(8,128)(2,1)}, bf16[2,4,192,128...) custom-call(bf16[32,384,128]{2,1,0:T(8,128)(2,1)} %encode_bulk.1.ref, ...), custom_call_target="tpu_custom_call" | custom-call | tf_op jit(solution)/shard_map/encode_head/pallas_call | solution.py:187
  32.7 1.6 collective-permute-start.16
  34.3 0.0 collective-permute-done.4.refs_6_
  34.3 0.6 collective-permute-start.2
  34.9 0.0 collective-permute-done.5.refs_7_
  34.9 2.8 %collective-permute-start.17 = (bf16[2,4,176,128]{3,2,1,0:T(8,128)(2,1)}, bf16[2,4,176,128]{3,2,1,0:T(8,128)(2,1)}, u32[]{:S(2)}, u32[]{:S(2)}) collective-permute-start(bf16[2,4,176,128]{3,2,1,0:T(8,128)(2,1)} %get-tuple-element.70), channel_id=1, source_target_pairs={{0,16},{8,24},{16,0},{24,8},{1,17},{9,25},{17,1},{25,9},{2,18},{10... | collective-permute-start | bytes 1081352 | tf_op jit(solution)/shard_map/ppermute | solution.py:507
  37.7 34.5 %collective-permute-done.16.refs_5_ = bf16[2,4,176,128]{3,2,1,0:T(8,128)(2,1)S(1)} collective-permute-done((bf16[2,4,176,128]{3,2,1,0:T(8,128)(2,1)}, bf16[2,4,176,128]{3,2,1,0:T(8,128)(2,1)S(1)}, u32[]{:S(2)}, u32[]{:S(2)}) %collective-permute-start.16) | collective-permute-done | bytes 360480 | tf_op jit(solution)/shard_map/ppermute | solution.py:507
  72.2 1.2 collective-permute-start.13
  73.4 1.2 collective-permute-start.14
  74.7 0.0 collective-permute-done.1.refs_2_
  74.7 1.1 collective-permute-start.15
  75.7 0.0 collective-permute-done.2.refs_3_
  75.7 2.1 %collective-permute-start.18 = (bf16[2,4,176,128]{3,2,1,0:T(8,128)(2,1)}, bf16[2,4,176,128]{3,2,1,0:T(8,128)(2,1)}, u32[]{:S(2)}, u32[]{:S(2)}) collective-permute-start(bf16[2,4,176,128]{3,2,1,0:T(8,128)(2,1)} %get-tuple-element.71), channel_id=1, source_target_pairs={{0,24},{8,0},{16,8},{24,16},{1,25},{9,1},{17,9},{25,17},{2,26},{10... | collective-permute-start | bytes 1081352 | tf_op jit(solution)/shard_map/ppermute | solution.py:507
  77.8 2.4 %sifted.2 = bf16[4,4,368,128]{3,2,1,0:T(8,128)(2,1)} custom-call(bf16[2,4,192,128]{3,2,1,0:T(8,128)(2,1)} %get-tuple-element.46.refs_0_, bf16[2,4,192,128]{3,2,1,0:T(8,128)(2,1)} %copy-done.1, bf16[2,4,192,128]{3,2,1,0:T(8,128)(2,1)} %collective-permute-done.1.refs_2_, bf16[2,4,192,128]{3,2,1,0:T(8,128)(2,1)} %collective-permute-done.2.refs_3_, ...), custom_call_target="tpu_custom_call" | custom-call | tf_op jit(solution)/shard_map/sifted/pallas_call | solution.py:220
  80.2 0.1 collective-permute-done.17.refs_6_
  80.3 0.1 collective-permute-start.6
  80.3 4.9 %collective-permute-done.18.refs_7_ = bf16[2,4,176,128]{3,2,1,0:T(8,128)(2,1)} collective-permute-done((bf16[2,4,176,128]{3,2,1,0:T(8,128)(2,1)}, bf16[2,4,176,128]{3,2,1,0:T(8,128)(2,1)}, u32[]{:S(2)}, u32[]{:S(2)}) %collective-permute-start.18) | collective-permute-done | bytes 360480 | tf_op jit(solution)/shard_map/ppermute | solution.py:507
  85.3 6.8 %collective-permute-done.13.refs_1_ = bf16[2,4,192,128]{3,2,1,0:T(8,128)(2,1)} collective-permute-done((bf16[2,4,192,128]{3,2,1,0:T(8,128)(2,1)}, bf16[2,4,192,128]{3,2,1,0:T(8,128)(2,1)}, u32[]{:S(2)}, u32[]{:S(2)}) %collective-permute-start.13) | collective-permute-done | bytes 393248 | tf_op jit(solution)/shard_map/ppermute | solution.py:507
  92.0 0.0 collective-permute-done.14.refs_2_
  92.0 1.9 %collective-permute-done.15.refs_3_ = bf16[2,4,192,128]{3,2,1,0:T(8,128)(2,1)} collective-permute-done((bf16[2,4,192,128]{3,2,1,0:T(8,128)(2,1)}, bf16[2,4,192,128]{3,2,1,0:T(8,128)(2,1)}, u32[]{:S(2)}, u32[]{:S(2)}) %collective-permute-start.15) | collective-permute-done | bytes 393248 | tf_op jit(solution)/shard_map/ppermute | solution.py:507
  93.9 2.4 %sifted.3 = bf16[4,4,368,128]{3,2,1,0:T(8,128)(2,1)} custom-call(bf16[2,4,192,128]{3,2,1,0:T(8,128)(2,1)} %get-tuple-element.64.refs_0_, bf16[2,4,192,128]{3,2,1,0:T(8,128)(2,1)} %collective-permute-done.13.refs_1_, bf16[2,4,192,128]{3,2,1,0:T(8,128)(2,1)} %collective-permute-done.14.refs_2_, bf16[2,4,192,128]{3,2,1,0:T(8,128)(2,1)} %collective-permute-done.15.refs_3_, ...), custom_call_target="tpu_custom_call" | custom-call | tf_op jit(solution)/shard_map/sifted/pallas_call | solution.py:220
  96.3 0.1 collective-permute-start.19
  96.4 0.0 collective-permute-done.6.got
  96.4 3.1 %crossed.2 = (bf16[2,4,192,128]{3,2,1,0:T(8,128)(2,1)}, bf16[2,4,192,128]{3,2,1,0:T(8,128)(2,1)}, bf16[2,4,192,128]{3,2,1,0:T(8,128)(2,1)}, bf16[2,4,192,128]{3,...) custom-call(bf16[4,4,368,128]{3,2,1,0:T(8,128)(2,1)} %collective-per, ...), custom_call_target="tpu_custom_call" | custom-call | tf_op jit(solution)/shard_map/crossed/pallas_call | solution.py:251
  99.5 1.1 collective-permute-start.10
  100.6 1.1 collective-permute-start.11
  101.8 0.9 collective-permute-start.12
  102.7 3.1 %crossed.3 = (bf16[2,4,192,128]{3,2,1,0:T(8,128)(2,1)}, bf16[2,4,192,128]{3,2,1,0:T(8,128)(2,1)}, bf16[2,4,192,128]{3,2,1,0:T(8,128)(2,1)}, bf16[2,4,192,128]{3,...) custom-call(bf16[4,4,368,128]{3,2,1,0:T(8,128)(2,1)} %collective-per, ...), custom_call_target="tpu_custom_call" | custom-call | tf_op jit(solution)/shard_map/crossed/pallas_call | solution.py:251
  105.8 1.2 collective-permute-start.23
  107.0 2.4 %collective-permute-start.24 = (bf16[2,4,176,128]{3,2,1,0:T(8,128)(2,1)}, bf16[2,4,176,128]{3,2,1,0:T(8,128)(2,1)S(1)}, u32[]{:S(2)}, u32[]{:S(2)}) collective-permute-start(bf16[2,4,176,128]{3,2,1,0:T(8,128)(2,1)} %get-tuple-element.78), channel_id=1, source_target_pairs={{0,4},{2,6},{4,0},{6,2},{1,5},{3,7},{5,1},{7,3},{8,12},{10,14},{12... | collective-permute-start | bytes 1081352 | tf_op jit(solution)/shard_map/ppermute | solution.py:507
  109.4 9.2 %collective-permute-done.10.refs_5_ = bf16[2,4,176,128]{3,2,1,0:T(8,128)(2,1)S(1)} collective-permute-done((bf16[2,4,176,128]{3,2,1,0:T(8,128)(2,1)}, bf16[2,4,176,128]{3,2,1,0:T(8,128)(2,1)S(1)}, u32[]{:S(2)}, u32[]{:S(2)}) %collective-permute-start.10) | collective-permute-done | bytes 360480 | tf_op jit(solution)/shard_map/ppermute | solution.py:507
  118.6 0.7 copy-done.4
  119.3 0.0 collective-permute-start.7
  119.3 0.0 collective-permute-done.11.refs_6_
  119.3 0.0 collective-permute-start.25
  119.3 1.7 collective-permute-done.12.refs_7_
  121.0 0.9 collective-permute-start.8
  121.9 4.4 %collective-permute-done.23.refs_5_ = bf16[2,4,176,128]{3,2,1,0:T(8,128)(2,1)S(1)} collective-permute-done((bf16[2,4,176,128]{3,2,1,0:T(8,128)(2,1)}, bf16[2,4,176,128]{3,2,1,0:T(8,128)(2,1)S(1)}, u32[]{:S(2)}, u32[]{:S(2)}) %collective-permute-start.23) | collective-permute-done | bytes 360480 | tf_op jit(solution)/shard_map/ppermute | solution.py:507
  126.3 0.7 collective-permute-start.9
  127.0 7.0 %collective-permute-done.24.refs_6_ = bf16[2,4,176,128]{3,2,1,0:T(8,128)(2,1)S(1)} collective-permute-done((bf16[2,4,176,128]{3,2,1,0:T(8,128)(2,1)}, bf16[2,4,176,128]{3,2,1,0:T(8,128)(2,1)S(1)}, u32[]{:S(2)}, u32[]{:S(2)}) %collective-permute-start.24) | collective-permute-done | bytes 360480 | tf_op jit(solution)/shard_map/ppermute | solution.py:507
  134.0 0.0 collective-permute-start.20
  134.0 1.7 collective-permute-done.25.refs_7_
  135.6 1.4 collective-permute-start.21
  137.1 0.9 collective-permute-start.22
  138.0 1.6 copy-done
  139.6 5.9 %decode_bulk.1 = (bf16[44,16,2048]{2,1,0:T(8,128)(2,1)}, f32[16,44]{1,0:T(8,128)}, bf16[16,2048]{1,0:T(8,128)(2,1)}) custom-call(bf16[16,2,384,128]{3,2,1,0:T(8,128)(2,1)} %bitcast.8), custom_call_target="tpu_custom_call" | custom-call | tf_op jit(solution)/shard_map/decode_bulk/pallas_call | solution.py:399
  145.6 2.0 %collective-permute-start.26 = (bf16[16,2048]{1,0:T(8,128)(2,1)}, bf16[16,2048]{1,0:T(8,128)(2,1)S(1)}, u32[]{:S(2)}, u32[]{:S(2)}) collective-permute-start(bf16[16,2048]{1,0:T(8,128)(2,1)} %get-tuple-element.84.refs_0_), channel_id=1, source_target_pairs={{0,32},{32,64},{64,96},{96,0},{1,33},{33,65},{65,97},{97,1},{2,34}... | collective-permute-start | bytes 196616 | tf_op jit(solution)/shard_map/ppermute | solution.py:507
  147.5 3.6 %collective-permute-start.27 = (bf16[16,2048]{1,0:T(8,128)(2,1)}, bf16[16,2048]{1,0:T(8,128)(2,1)S(1)}, u32[]{:S(2)}, u32[]{:S(2)}) collective-permute-start(bf16[16,2048]{1,0:T(8,128)(2,1)} %get-tuple-element.84.refs_0_), channel_id=1, source_target_pairs={{0,64},{32,96},{64,0},{96,32},{1,65},{33,97},{65,1},{97,33},{2,66}... | collective-permute-start | bytes 196616 | tf_op jit(solution)/shard_map/ppermute | solution.py:507
  151.1 3.5 %collective-permute-done.20.refs_1_ = bf16[2,4,192,128]{3,2,1,0:T(8,128)(2,1)} collective-permute-done((bf16[2,4,192,128]{3,2,1,0:T(8,128)(2,1)}, bf16[2,4,192,128]{3,2,1,0:T(8,128)(2,1)}, u32[]{:S(2)}, u32[]{:S(2)}) %collective-permute-start.20) | collective-permute-done | bytes 393248 | tf_op jit(solution)/shard_map/ppermute | solution.py:507
  154.7 4.0 %collective-permute-start.28 = (bf16[16,2048]{1,0:T(8,128)(2,1)}, bf16[16,2048]{1,0:T(8,128)(2,1)S(1)}, u32[]{:S(2)}, u32[]{:S(2)}) collective-permute-start(bf16[16,2048]{1,0:T(8,128)(2,1)} %get-tuple-element.84.refs_0_), channel_id=1, source_target_pairs={{0,96},{32,0},{64,32},{96,64},{1,97},{33,1},{65,33},{97,65},{2,98}... | collective-permute-start | bytes 196616 | tf_op jit(solution)/shard_map/ppermute | solution.py:507
  158.7 6.3 %decode_head.2 = (bf16[44,16,2048]{2,1,0:T(8,128)(2,1)}, f32[16,44]{1,0:T(8,128)}) custom-call(bf16[2,4,192,128]{3,2,1,0:T(8,128)(2,1)} %get-tuple-element.54.refs_0_, bf16[2,4,192,128]{3,2,1,0:T(8,128)(2,1)} %copy-done.3, bf16[2,4,192,128]{3,2,1,0:T(8,128)(2,1)} %collective-permute-done.8.refs_2_, bf16[2,4,192,128]{3,2,1,0:T(8,128)(2,1)} %collective-permute-done.9.refs_3_, ...), custom_call_target="tpu_custom_call" | custom-call | tf_op jit(solution)/shard_map/decode_head/pallas_call | solution.py:470
  165.0 6.3 %decode_head.3 = (bf16[44,16,2048]{2,1,0:T(8,128)(2,1)}, f32[16,44]{1,0:T(8,128)}) custom-call(bf16[2,4,192,128]{3,2,1,0:T(8,128)(2,1)} %get-tuple-element.72.refs_0_, bf16[2,4,192,128]{3,2,1,0:T(8,128)(2,1)} %collective-permute-done.20.refs_1_, bf16[2,4,192,128]{3,2,1,0:T(8,128)(2,1)} %collective-permute-done.21.refs_2_, ...), custom_call_target="tpu_custom_call" | custom-call | tf_op jit(solution)/shard_map/decode_head/pallas_call | solution.py:470
  171.4 0.6 copy-done.8
  172.0 0.0 copy-done.9
  172.0 0.6 copy-done.10
  172.6 1.7 joined.1
  (29 shorter events, 0.1 us)
Async XLA Ops:
  6.5 26.2 %collective-permute-start.3 = (bf16[2,4,176,128]{3,2,1,0:T(8,128)(2,1)}, bf16[2,4,176,128]{3,2,1,0:T(8,128)(2,1)}, u32[]{:S(2)}, u32[]{:S(2)}) collective-permute-start(bf16[2,4,176,128]{3,2,1,0:T(8,128)(2,1)} %get-tuple-element.51), channel_id=1, source_target_pairs={{0,8},{8,16},{16,24},{24,0},{1,9},{9,17},{17,25},{25,1},{2,10},{10... | collective-permute-start | bytes 1081352 | tf_op jit(solution)/shard_map/ppermute | solution.py:507
  8.1 26.2 %collective-permute-start.4 = (bf16[2,4,176,128]{3,2,1,0:T(8,128)(2,1)}, bf16[2,4,176,128]{3,2,1,0:T(8,128)(2,1)}, u32[]{:S(2)}, u32[]{:S(2)}) collective-permute-start(bf16[2,4,176,128]{3,2,1,0:T(8,128)(2,1)} %get-tuple-element.52), channel_id=1, source_target_pairs={{0,16},{8,24},{16,0},{24,8},{1,17},{9,25},{17,1},{25,9},{2,18},{10... | collective-permute-start | bytes 1081352 | tf_op jit(solution)/shard_map/ppermute | solution.py:507
  11.0 23.8 %collective-permute-start.5 = (bf16[2,4,176,128]{3,2,1,0:T(8,128)(2,1)}, bf16[2,4,176,128]{3,2,1,0:T(8,128)(2,1)}, u32[]{:S(2)}, u32[]{:S(2)}) collective-permute-start(bf16[2,4,176,128]{3,2,1,0:T(8,128)(2,1)} %get-tuple-element.53), channel_id=1, source_target_pairs={{0,24},{8,0},{16,8},{24,16},{1,25},{9,1},{17,9},{25,17},{2,26},{10... | collective-permute-start | bytes 1081352 | tf_op jit(solution)/shard_map/ppermute | solution.py:507
  12.4 61.0 %collective-permute-start = (bf16[2,4,192,128]{3,2,1,0:T(8,128)(2,1)}, bf16[2,4,192,128]{3,2,1,0:T(8,128)(2,1)S(1)}, u32[]{:S(2)}, u32[]{:S(2)}) collective-permute-start(bf16[2,4,192,128]{3,2,1,0:T(8,128)(2,1)} %get-tuple-element.47), channel_id=1, source_target_pairs={{0,2},{2,4},{4,6},{6,0},{1,3},{3,5},{5,7},{7,1},{8,10},{10,12},{12... | collective-permute-start | bytes 1179656 | tf_op jit(solution)/shard_map/ppermute | solution.py:507
  13.6 61.1 %collective-permute-start.1 = (bf16[2,4,192,128]{3,2,1,0:T(8,128)(2,1)}, bf16[2,4,192,128]{3,2,1,0:T(8,128)(2,1)}, u32[]{:S(2)}, u32[]{:S(2)}) collective-permute-start(bf16[2,4,192,128]{3,2,1,0:T(8,128)(2,1)} %get-tuple-element.48), channel_id=1, source_target_pairs={{0,4},{2,6},{4,0},{6,2},{1,5},{3,7},{5,1},{7,3},{8,12},{10,14},{12... | collective-permute-start | bytes 1179656 | tf_op jit(solution)/shard_map/ppermute | solution.py:507
  20.4 117.6 %all-to-all-start = ((bf16[32,384,128]{2,1,0:T(8,128)(2,1)}), bf16[32,384,128]{2,1,0:T(8,128)(2,1)S(1)}, u32[]{:S(2)}, u32[]{:S(2)}) async-start(bf16[32,384,128]{2,1,0:T(8,128)(2,1)} %encode_bulk.1.refs_0_), calls=%async_computation | async-start | bytes 6291456 | tf_op jit(solution)/shard_map/all_to_all | solution.py:532
  32.7 39.5 %collective-permute-start.16 = (bf16[2,4,176,128]{3,2,1,0:T(8,128)(2,1)}, bf16[2,4,176,128]{3,2,1,0:T(8,128)(2,1)S(1)}, u32[]{:S(2)}, u32[]{:S(2)}) collective-permute-start(bf16[2,4,176,128]{3,2,1,0:T(8,128)(2,1)} %get-tuple-element.69), channel_id=1, source_target_pairs={{0,8},{8,16},{16,24},{24,0},{1,9},{9,17},{17,25},{25,1},{2,10},{10... | collective-permute-start | bytes 1081352 | tf_op jit(solution)/shard_map/ppermute | solution.py:507
  34.3 41.4 %collective-permute-start.2 = (bf16[2,4,192,128]{3,2,1,0:T(8,128)(2,1)}, bf16[2,4,192,128]{3,2,1,0:T(8,128)(2,1)}, u32[]{:S(2)}, u32[]{:S(2)}) collective-permute-start(bf16[2,4,192,128]{3,2,1,0:T(8,128)(2,1)} %get-tuple-element.49), channel_id=1, source_target_pairs={{0,6},{2,0},{4,2},{6,4},{1,7},{3,1},{5,3},{7,5},{8,14},{10,8},{12,... | collective-permute-start | bytes 1179656 | tf_op jit(solution)/shard_map/ppermute | solution.py:507
  34.9 45.4 %collective-permute-start.17 = (bf16[2,4,176,128]{3,2,1,0:T(8,128)(2,1)}, bf16[2,4,176,128]{3,2,1,0:T(8,128)(2,1)}, u32[]{:S(2)}, u32[]{:S(2)}) collective-permute-start(bf16[2,4,176,128]{3,2,1,0:T(8,128)(2,1)} %get-tuple-element.70), channel_id=1, source_target_pairs={{0,16},{8,24},{16,0},{24,8},{1,17},{9,25},{17,1},{25,9},{2,18},{10... | collective-permute-start | bytes 1081352 | tf_op jit(solution)/shard_map/ppermute | solution.py:507
  72.2 1.2 copy-start.2
  72.2 19.8 %collective-permute-start.13 = (bf16[2,4,192,128]{3,2,1,0:T(8,128)(2,1)}, bf16[2,4,192,128]{3,2,1,0:T(8,128)(2,1)}, u32[]{:S(2)}, u32[]{:S(2)}) collective-permute-start(bf16[2,4,192,128]{3,2,1,0:T(8,128)(2,1)} %get-tuple-element.65), channel_id=1, source_target_pairs={{0,2},{2,4},{4,6},{6,0},{1,3},{3,5},{5,7},{7,1},{8,10},{10,12},{12... | collective-permute-start | bytes 1179656 | tf_op jit(solution)/shard_map/ppermute | solution.py:507
  73.4 4.4 %copy-start.1 = (bf16[2,4,192,128]{3,2,1,0:T(8,128)(2,1)}, bf16[2,4,192,128]{3,2,1,0:T(8,128)(2,1)S(1)}, u32[]{:S(2)}) copy-start(bf16[2,4,192,128]{3,2,1,0:T(8,128)(2,1)S(1)} %collective-permute-done.refs_1_) | copy-start | bytes 1179652
  73.4 18.6 %collective-permute-start.14 = (bf16[2,4,192,128]{3,2,1,0:T(8,128)(2,1)}, bf16[2,4,192,128]{3,2,1,0:T(8,128)(2,1)}, u32[]{:S(2)}, u32[]{:S(2)}) collective-permute-start(bf16[2,4,192,128]{3,2,1,0:T(8,128)(2,1)} %get-tuple-element.66), channel_id=1, source_target_pairs={{0,4},{2,6},{4,0},{6,2},{1,5},{3,7},{5,1},{7,3},{8,12},{10,14},{12... | collective-permute-start | bytes 1179656 | tf_op jit(solution)/shard_map/ppermute | solution.py:507
  74.7 19.3 %collective-permute-start.15 = (bf16[2,4,192,128]{3,2,1,0:T(8,128)(2,1)}, bf16[2,4,192,128]{3,2,1,0:T(8,128)(2,1)}, u32[]{:S(2)}, u32[]{:S(2)}) collective-permute-start(bf16[2,4,192,128]{3,2,1,0:T(8,128)(2,1)} %get-tuple-element.67), channel_id=1, source_target_pairs={{0,6},{2,0},{4,2},{6,4},{1,7},{3,1},{5,3},{7,5},{8,14},{10,8},{12,... | collective-permute-start | bytes 1179656 | tf_op jit(solution)/shard_map/ppermute | solution.py:507
  75.7 9.6 %collective-permute-start.18 = (bf16[2,4,176,128]{3,2,1,0:T(8,128)(2,1)}, bf16[2,4,176,128]{3,2,1,0:T(8,128)(2,1)}, u32[]{:S(2)}, u32[]{:S(2)}) collective-permute-start(bf16[2,4,176,128]{3,2,1,0:T(8,128)(2,1)} %get-tuple-element.71), channel_id=1, source_target_pairs={{0,24},{8,0},{16,8},{24,16},{1,25},{9,1},{17,9},{25,17},{2,26},{10... | collective-permute-start | bytes 1081352 | tf_op jit(solution)/shard_map/ppermute | solution.py:507
  80.3 16.1 %collective-permute-start.6 = (bf16[4,4,368,128]{3,2,1,0:T(8,128)(2,1)}, bf16[4,4,368,128]{3,2,1,0:T(8,128)(2,1)}, u32[]{:S(2)}, u32[]{:S(2)}) collective-permute-start(bf16[4,4,368,128]{3,2,1,0:T(8,128)(2,1)} %sifted.2), channel_id=1, source_target_pairs={{0,1},{1,0},{2,3},{3,2},{4,5},{5,4},{6,7},{7,6},{8,9},{9,8},{10,11... | collective-permute-start | bytes 4521992 | tf_op jit(solution)/shard_map/ppermute | solution.py:526
  96.3 6.4 %collective-permute-start.19 = (bf16[4,4,368,128]{3,2,1,0:T(8,128)(2,1)}, bf16[4,4,368,128]{3,2,1,0:T(8,128)(2,1)}, u32[]{:S(2)}, u32[]{:S(2)}) collective-permute-start(bf16[4,4,368,128]{3,2,1,0:T(8,128)(2,1)} %sifted.3), channel_id=1, source_target_pairs={{0,1},{1,0},{2,3},{3,2},{4,5},{5,4},{6,7},{7,6},{8,9},{9,8},{10,11... | collective-permute-start | bytes 4521992 | tf_op jit(solution)/shard_map/ppermute | solution.py:526
  99.5 19.1 %collective-permute-start.10 = (bf16[2,4,176,128]{3,2,1,0:T(8,128)(2,1)}, bf16[2,4,176,128]{3,2,1,0:T(8,128)(2,1)S(1)}, u32[]{:S(2)}, u32[]{:S(2)}) collective-permute-start(bf16[2,4,176,128]{3,2,1,0:T(8,128)(2,1)} %get-tuple-element.59), channel_id=1, source_target_pairs={{0,2},{2,4},{4,6},{6,0},{1,3},{3,5},{5,7},{7,1},{8,10},{10,12},{12... | collective-permute-start | bytes 1081352 | tf_op jit(solution)/shard_map/ppermute | solution.py:507
  100.6 18.7 %collective-permute-start.11 = (bf16[2,4,176,128]{3,2,1,0:T(8,128)(2,1)}, bf16[2,4,176,128]{3,2,1,0:T(8,128)(2,1)}, u32[]{:S(2)}, u32[]{:S(2)}) collective-permute-start(bf16[2,4,176,128]{3,2,1,0:T(8,128)(2,1)} %get-tuple-element.60), channel_id=1, source_target_pairs={{0,4},{2,6},{4,0},{6,2},{1,5},{3,7},{5,1},{7,3},{8,12},{10,14},{12... | collective-permute-start | bytes 1081352 | tf_op jit(solution)/shard_map/ppermute | solution.py:507
  101.8 19.2 %collective-permute-start.12 = (bf16[2,4,176,128]{3,2,1,0:T(8,128)(2,1)}, bf16[2,4,176,128]{3,2,1,0:T(8,128)(2,1)}, u32[]{:S(2)}, u32[]{:S(2)}) collective-permute-start(bf16[2,4,176,128]{3,2,1,0:T(8,128)(2,1)} %get-tuple-element.61), channel_id=1, source_target_pairs={{0,6},{2,0},{4,2},{6,4},{1,7},{3,1},{5,3},{7,5},{8,14},{10,8},{12,... | collective-permute-start | bytes 1081352 | tf_op jit(solution)/shard_map/ppermute | solution.py:507
  105.8 20.5 %collective-permute-start.23 = (bf16[2,4,176,128]{3,2,1,0:T(8,128)(2,1)}, bf16[2,4,176,128]{3,2,1,0:T(8,128)(2,1)S(1)}, u32[]{:S(2)}, u32[]{:S(2)}) collective-permute-start(bf16[2,4,176,128]{3,2,1,0:T(8,128)(2,1)} %get-tuple-element.77), channel_id=1, source_target_pairs={{0,2},{2,4},{4,6},{6,0},{1,3},{3,5},{5,7},{7,1},{8,10},{10,12},{12... | collective-permute-start | bytes 1081352 | tf_op jit(solution)/shard_map/ppermute | solution.py:507
  107.0 27.0 %collective-permute-start.24 = (bf16[2,4,176,128]{3,2,1,0:T(8,128)(2,1)}, bf16[2,4,176,128]{3,2,1,0:T(8,128)(2,1)S(1)}, u32[]{:S(2)}, u32[]{:S(2)}) collective-permute-start(bf16[2,4,176,128]{3,2,1,0:T(8,128)(2,1)} %get-tuple-element.78), channel_id=1, source_target_pairs={{0,4},{2,6},{4,0},{6,2},{1,5},{3,7},{5,1},{7,3},{8,12},{10,14},{12... | collective-permute-start | bytes 1081352 | tf_op jit(solution)/shard_map/ppermute | solution.py:507
  118.6 0.7 copy-start.4
  119.3 17.7 %collective-permute-start.7 = (bf16[2,4,192,128]{3,2,1,0:T(8,128)(2,1)}, bf16[2,4,192,128]{3,2,1,0:T(8,128)(2,1)S(1)}, u32[]{:S(2)}, u32[]{:S(2)}) collective-permute-start(bf16[2,4,192,128]{3,2,1,0:T(8,128)(2,1)} %get-tuple-element.55), channel_id=1, source_target_pairs={{0,8},{8,16},{16,24},{24,0},{1,9},{9,17},{17,25},{25,1},{2,10},{10... | collective-permute-start | bytes 1179656 | tf_op jit(solution)/shard_map/ppermute | solution.py:507
  119.3 16.3 %collective-permute-start.25 = (bf16[2,4,176,128]{3,2,1,0:T(8,128)(2,1)}, bf16[2,4,176,128]{3,2,1,0:T(8,128)(2,1)S(1)}, u32[]{:S(2)}, u32[]{:S(2)}) collective-permute-start(bf16[2,4,176,128]{3,2,1,0:T(8,128)(2,1)} %get-tuple-element.79), channel_id=1, source_target_pairs={{0,6},{2,0},{4,2},{6,4},{1,7},{3,1},{5,3},{7,5},{8,14},{10,8},{12,... | collective-permute-start | bytes 1081352 | tf_op jit(solution)/shard_map/ppermute | solution.py:507
  121.0 24.5 %collective-permute-start.8 = (bf16[2,4,192,128]{3,2,1,0:T(8,128)(2,1)}, bf16[2,4,192,128]{3,2,1,0:T(8,128)(2,1)}, u32[]{:S(2)}, u32[]{:S(2)}) collective-permute-start(bf16[2,4,192,128]{3,2,1,0:T(8,128)(2,1)} %get-tuple-element.56), channel_id=1, source_target_pairs={{0,16},{8,24},{16,0},{24,8},{1,17},{9,25},{17,1},{25,9},{2,18},{10... | collective-permute-start | bytes 1179656 | tf_op jit(solution)/shard_map/ppermute | solution.py:507
  126.3 10.7 %copy-start.5 = (bf16[2,4,176,128]{3,2,1,0:T(8,128)(2,1)}, bf16[2,4,176,128]{3,2,1,0:T(8,128)(2,1)S(1)}, u32[]{:S(2)}) copy-start(bf16[2,4,176,128]{3,2,1,0:T(8,128)(2,1)S(1)} %collective-permute-done.23.refs_5_) | copy-start | bytes 1081348
  126.3 21.2 %collective-permute-start.9 = (bf16[2,4,192,128]{3,2,1,0:T(8,128)(2,1)}, bf16[2,4,192,128]{3,2,1,0:T(8,128)(2,1)}, u32[]{:S(2)}, u32[]{:S(2)}) collective-permute-start(bf16[2,4,192,128]{3,2,1,0:T(8,128)(2,1)} %get-tuple-element.57), channel_id=1, source_target_pairs={{0,24},{8,0},{16,8},{24,16},{1,25},{9,1},{17,9},{25,17},{2,26},{10... | collective-permute-start | bytes 1179656 | tf_op jit(solution)/shard_map/ppermute | solution.py:507
  134.0 3.1 %copy-start.6 = (bf16[2,4,176,128]{3,2,1,0:T(8,128)(2,1)}, bf16[2,4,176,128]{3,2,1,0:T(8,128)(2,1)S(1)}, u32[]{:S(2)}) copy-start(bf16[2,4,176,128]{3,2,1,0:T(8,128)(2,1)S(1)} %collective-permute-done.24.refs_6_) | copy-start | bytes 1081348
  134.0 20.7 %collective-permute-start.20 = (bf16[2,4,192,128]{3,2,1,0:T(8,128)(2,1)}, bf16[2,4,192,128]{3,2,1,0:T(8,128)(2,1)}, u32[]{:S(2)}, u32[]{:S(2)}) collective-permute-start(bf16[2,4,192,128]{3,2,1,0:T(8,128)(2,1)} %get-tuple-element.73), channel_id=1, source_target_pairs={{0,8},{8,16},{16,24},{24,0},{1,9},{9,17},{17,25},{25,1},{2,10},{10... | collective-permute-start | bytes 1179656 | tf_op jit(solution)/shard_map/ppermute | solution.py:507
  135.6 1.4 copy-start.7
  135.6 29.4 %collective-permute-start.21 = (bf16[2,4,192,128]{3,2,1,0:T(8,128)(2,1)}, bf16[2,4,192,128]{3,2,1,0:T(8,128)(2,1)}, u32[]{:S(2)}, u32[]{:S(2)}) collective-permute-start(bf16[2,4,192,128]{3,2,1,0:T(8,128)(2,1)} %get-tuple-element.74), channel_id=1, source_target_pairs={{0,16},{8,24},{16,0},{24,8},{1,17},{9,25},{17,1},{25,9},{2,18},{10... | collective-permute-start | bytes 1179656 | tf_op jit(solution)/shard_map/ppermute | solution.py:507
  137.0 21.7 %copy-start.3 = (bf16[2,4,192,128]{3,2,1,0:T(8,128)(2,1)}, bf16[2,4,192,128]{3,2,1,0:T(8,128)(2,1)S(1)}, u32[]{:S(2)}) copy-start(bf16[2,4,192,128]{3,2,1,0:T(8,128)(2,1)S(1)} %collective-permute-done.7.refs_1_) | copy-start | bytes 1179652
  137.1 28.0 %collective-permute-start.22 = (bf16[2,4,192,128]{3,2,1,0:T(8,128)(2,1)}, bf16[2,4,192,128]{3,2,1,0:T(8,128)(2,1)}, u32[]{:S(2)}, u32[]{:S(2)}) collective-permute-start(bf16[2,4,192,128]{3,2,1,0:T(8,128)(2,1)} %get-tuple-element.75), channel_id=1, source_target_pairs={{0,24},{8,0},{16,8},{24,16},{1,25},{9,1},{17,9},{25,17},{2,26},{10... | collective-permute-start | bytes 1179656 | tf_op jit(solution)/shard_map/ppermute | solution.py:507
  138.0 1.6 copy-start
  145.6 25.8 %collective-permute-start.26 = (bf16[16,2048]{1,0:T(8,128)(2,1)}, bf16[16,2048]{1,0:T(8,128)(2,1)S(1)}, u32[]{:S(2)}, u32[]{:S(2)}) collective-permute-start(bf16[16,2048]{1,0:T(8,128)(2,1)} %get-tuple-element.84.refs_0_), channel_id=1, source_target_pairs={{0,32},{32,64},{64,96},{96,0},{1,33},{33,65},{65,97},{97,1},{2,34}... | collective-permute-start | bytes 196616 | tf_op jit(solution)/shard_map/ppermute | solution.py:507
  147.5 23.8 %collective-permute-start.27 = (bf16[16,2048]{1,0:T(8,128)(2,1)}, bf16[16,2048]{1,0:T(8,128)(2,1)S(1)}, u32[]{:S(2)}, u32[]{:S(2)}) collective-permute-start(bf16[16,2048]{1,0:T(8,128)(2,1)} %get-tuple-element.84.refs_0_), channel_id=1, source_target_pairs={{0,64},{32,96},{64,0},{96,32},{1,65},{33,97},{65,1},{97,33},{2,66}... | collective-permute-start | bytes 196616 | tf_op jit(solution)/shard_map/ppermute | solution.py:507
  154.7 16.7 %collective-permute-start.28 = (bf16[16,2048]{1,0:T(8,128)(2,1)}, bf16[16,2048]{1,0:T(8,128)(2,1)S(1)}, u32[]{:S(2)}, u32[]{:S(2)}) collective-permute-start(bf16[16,2048]{1,0:T(8,128)(2,1)} %get-tuple-element.84.refs_0_), channel_id=1, source_target_pairs={{0,96},{32,0},{64,32},{96,64},{1,97},{33,1},{65,33},{97,65},{2,98}... | collective-permute-start | bytes 196616 | tf_op jit(solution)/shard_map/ppermute | solution.py:507
  171.3 0.6 copy-start.8
  171.3 0.6 copy-start.9
  172.0 0.6 copy-start.10

commit v2 on v1

--- a/solution.py
+++ b/solution.py
@@ -58,9 +58,8 @@
 
     lax.fori_loop(0, depth, first, 0)
 
-    def tile_of(i, carry):
+    def coded(i, at_stage):
         slot = lax.rem(i, depth)
-        landed(xin.at[slot], sem_in.at[slot])
         at = rows_at(i * LANES, LANES, LANES)
         for e in range(half):
             a, b = xin[slot, e + half * odd], xin[slot, e + half * (1 - odd)]
@@ -75,17 +74,32 @@
             v4 = v2 * v2
             v8 = v4 * v4
             y = v8 * v8 * v
-            stage[pl.ds(e, LANES, stride=half), :] = y.T
-        pay[rows_at(i * LANES * half, LANES * half, LANES * half), :] = stage[...].astype(jnp.bfloat16)
-
-        @pl.when(i + depth < tiles)
-        def _():
-            fetch(i + depth)
-
-        after(i)
+            at_stage[pl.ds(e, LANES, stride=half), :] = y.T
+
+    def several(i, stages):
+        for k in range(len(stages)):
+            slot = lax.rem(i + k, depth)
+            landed(xin.at[slot], sem_in.at[slot])
+        for k, at_stage in enumerate(stages):
+            coded(i + k, at_stage)
+        for k, at_stage in enumerate(stages):
+            rows = rows_at((i + k) * LANES * half, LANES * half, LANES * half)
+            pay[rows, :] = at_stage[...].astype(jnp.bfloat16)
+        for k in range(len(stages)):
+
+            @pl.when(i + k + depth < tiles)
+            def _():
+                fetch(i + k + depth)
+
+            after(i + k)
+
+    def pair_of(m, carry):
+        several(2 * m, stage)
         return carry
 
-    lax.fori_loop(0, tiles, tile_of, 0)
+    lax.fori_loop(0, tiles // 2, pair_of, 0)
+    for i in range(tiles // 2 * 2, tiles):
+        several(i, stage[:1])
     total = sums[...]
     total = jnp.where(odd == 1, jnp.concatenate([total[half:], total[:half]], 0), total)
     high = total.astype(jnp.bfloat16).astype(jnp.float32)
@@ -99,7 +113,7 @@
 def encode_scratch(peers, experts, rows, columns, depth):
     return [
         pltpu.VMEM((depth, experts, rows, LANES), jnp.float32),
-        pltpu.VMEM((LANES * experts // 2, LANES), jnp.float32),
+        [pltpu.VMEM((LANES * experts // 2, LANES), jnp.float32)] * 2,
         pltpu.VMEM((columns * experts // 2, LANES), jnp.bfloat16),
         pltpu.VMEM((experts, columns), jnp.float32),
         pltpu.VMEM((peers, experts, LANES), jnp.bfloat16),
@@ -118,8 +132,13 @@
     block = share * half
 
     if routed:
-        weight, gain = refs[1:3]
-        router, sem_router = refs[10 + 2 * routed :]
+        router, sem_router, weight, gain, sem_small = refs[10 + 2 * routed :]
+        for k, small in enumerate((weight, gain)):
+            pltpu.make_async_copy(refs[1 + k], small, sem_small.at[k]).start()
+
+    def add_router():
+        for k, small in enumerate((weight, gain)):
+            landed(small, sem_small.at[k])
         part = weight[...] * gain[...]
         part = jnp.where(lax.axis_index("core") == 1, jnp.concatenate([part[half:], part[:half]], 0), part)
         part = jnp.concatenate([part[:half], part[half:]], 1)
@@ -138,6 +157,8 @@
         lax.fori_loop(tile * LANES // share, (tile + 1) * LANES // share, send, 0)
 
     encode_tiles(x, xin, stage, pay, sums, notes, sem_in, peers, tiles, after)
+    if routed:
+        add_router()
     pltpu.make_async_copy(notes, out.at[:, pl.ds(block, experts), :], sem_note).start()
     landed(pay, sem_pay)
     landed(notes, sem_note)
@@ -151,11 +172,13 @@
     height = columns // peers * experts // 2 + experts * (1 + routed)
     return pl.pallas_call(
         behind(len(ahead), functools.partial(encode_bulk_kernel, routed, peers, columns // LANES)),
-        in_specs=anywhere(len(ahead) + 1) + [pl.BlockSpec(memory_space=pltpu.VMEM)] * len(small),
+        in_specs=anywhere(len(ahead) + 1 + len(small)),
         out_specs=pl.BlockSpec(memory_space=pl.ANY),
         out_shape=jax.ShapeDtypeStruct((peers, height, LANES), jnp.bfloat16),
         scratch_shapes=encode_scratch(peers, experts, rows, columns, depth)
-        + [pltpu.VMEM((peers, experts, LANES), jnp.bfloat16), pltpu.SemaphoreType.DMA] * routed,
+        + [pltpu.VMEM((peers, experts, LANES), jnp.bfloat16), pltpu.SemaphoreType.DMA] * routed
+        + [pltpu.VMEM(a.shape, a.dtype) for a in small]
+        + [pltpu.SemaphoreType.DMA((2,))] * routed,
         name="encode_bulk",
     )(*ahead, x, *small)
 
@@ -415,7 +438,7 @@
 
 def decode_head_kernel(*refs):
     by_x, by_y, refs = refs[:SIDE], refs[SIDE : 2 * SIDE], refs[2 * SIDE :]
-    ready_out, scale_out, *refs = refs
+    ready_out, scale_to, scale_out, sem_scale, *refs = refs
     held_x, held_y, notes, sem_in, sem_note, factors, turned, ready_factors, picks, ready, sem_out = refs
     experts, share = scale_out.shape
     half = experts // 2
@@ -441,6 +464,7 @@
                 rows = pl.ds((steps - turn) * height, experts)
                 notes[SIDE * dx + dy, which] = held_y[dx, even[which], dy, rows, :]
     factors_from(notes, scale_out, factors, turned, ready_factors)
+    pltpu.make_async_copy(scale_out, scale_to, sem_scale).start()
 
     def place(q):
         return chip_at(SIDE - q // SIDE, SIDE - q % SIDE)
@@ -461,18 +485,19 @@
 
     lax.fori_loop(0, turn, step_with(held_x, 0), 0)
     lax.fori_loop(turn, steps, step_with(held_y, turn), 0)
+    landed(scale_out, sem_scale)
     for slot in range(ready.shape[0]):
         landed(ready.at[slot], sem_out.at[slot])
 
 
 def decode_head(parts, experts, share, rows, outs=6):
-    vmem = pl.BlockSpec(memory_space=pltpu.VMEM)
     return pl.pallas_call(
         decode_head_kernel,
         in_specs=anywhere(len(parts)),
-        out_specs=anywhere(1) + [vmem],
+        out_specs=anywhere(2),
         out_shape=decoded_shapes(experts, share, rows),
-        scratch_shapes=[pltpu.VMEM((SIDE, *parts[k].shape), jnp.bfloat16) for k in (0, SIDE)]
+        scratch_shapes=[pltpu.VMEM((experts, share), jnp.float32), pltpu.SemaphoreType.DMA]
+        + [pltpu.VMEM((SIDE, *parts[k].shape), jnp.bfloat16) for k in (0, SIDE)]
         + [
             pltpu.VMEM((CHIPS, 2, experts, LANES), jnp.bfloat16),
             pltpu.SemaphoreType.DMA((share // STEP,)),

time: 175 us -> 172 us (0.983)
  Pallas kernels: 48.8 us -> 46.2 us
  transfers between devices with their start and end apart: 30 -> 30, of which waited for: 11 -> 12; matrix products, arithmetic and copies ran while one was open for 0% -> 0% of each run, Pallas kernels for 24% -> 23%
where the time goes in v2:
time: 172 us
  waiting for transfers between devices  75.3 us (44%)
  Pallas kernels  46.2 us (27%)
  starting transfers between devices  45.8 us (27%)
  local copies, waits for them, and re-layouts  3.65 us (2%)
    ppermute x27, waiting for transfers between devices, moved(): lax.ppermute(value, axis, [(k, (k + shift) % SIDE) for k in range(SIDE)])  75.3 us
    ppermute x27, starting transfers between devices, moved(): lax.ppermute(value, axis, [(k, (k + shift) % SIDE) for k in range(SIDE)])  39.3 us
    pallas_call x2, Pallas kernels, decode_head(): pl.pallas_call(decode_head_kernel, in_specs=anywhere(len(parts)), out_spe...  11.4 us
    pallas_call x2, Pallas kernels, encode_head(): pl.pallas_call(behind(len(ahead), functools.partial(encode_head_kernel, p...  11.2 us
    all_to_all x1, starting transfers between devices, body(): arrived = lax.all_to_all(first, PLANE, 0, 0, tiled=True)  6.48 us
    pallas_call x2, Pallas kernels, crossed(): pl.pallas_call(cross_kernel, in_specs=anywhere(1 + 2 * SIDE), out_specs=a...  6.2 us
    pallas_call x1, Pallas kernels, decode_bulk(): pl.pallas_call(functools.partial(decode_bulk_kernel, depth), in_specs=any...  5.91 us
    pallas_call x1, Pallas kernels, encode_bulk(): pl.pallas_call(behind(len(ahead), functools.partial(encode_bulk_kernel, r...  5.15 us
  transfers between devices with their start and end apart: 30, of which 12 were waited for; matrix products, arithmetic and copies ran while one was open for 0% of the time, Pallas kernels for 23%

profile of v2, /device:TPU:4, one launch (start us, length us, event | category | flops | bytes accessed | tf_op | source)
XLA Modules:
  0.0 171.9 jit_solution(7956750449077290034)
XLA Ops:
  0.6 5.6 %encode_head.2 = (bf16[2,4,192,128]{3,2,1,0:T(8,128)(2,1)}, bf16[2,4,192,128]{3,2,1,0:T(8,128)(2,1)}, bf16[2,4,192,128]{3,2,1,0:T(8,128)(2,1)}, bf16[2,4,192,128...) custom-call(f32[16,64,1408]{2,1,0:T(8,128)} %refs_0_.1), custom_call_target="tpu_custom_call" | custom-call | tf_op jit(solution)/shard_map/encode_head/pallas_call | solution.py:210
  6.2 1.6 collective-permute-start.3
  7.9 2.9 %collective-permute-start.4 = (bf16[2,4,176,128]{3,2,1,0:T(8,128)(2,1)}, bf16[2,4,176,128]{3,2,1,0:T(8,128)(2,1)}, u32[]{:S(2)}, u32[]{:S(2)}) collective-permute-start(bf16[2,4,176,128]{3,2,1,0:T(8,128)(2,1)} %get-tuple-element.52), channel_id=1, source_target_pairs={{0,16},{8,24},{16,0},{24,8},{1,17},{9,25},{17,1},{25,9},{2,18},{10... | collective-permute-start | bytes 1081352 | tf_op jit(solution)/shard_map/ppermute | solution.py:532
  10.8 1.3 collective-permute-start.5
  12.1 1.2 collective-permute-start
  13.3 0.8 collective-permute-start.1
  14.1 5.1 %encode_bulk.1.refs_0_ = bf16[32,384,128]{2,1,0:T(8,128)(2,1)} custom-call(bf16[2,4,192,128]{3,2,1,0:T(8,128)(2,1)} %get-tuple-element.46.refs_0_, f32[16,64,1408]{2,1,0:T(8,128)} %refs_1_.1, f32[16,64]{1,0:T(8,128)} %bitcast.11, f32[1,64]{1,0:T(1,128)} %bitcast.12), custom_call_target="tpu_custom_call" | custom-call | tf_op jit(solution)/shard_map/encode_bulk/pallas_call | solution.py:173
  19.3 6.5 %all-to-all-start = ((bf16[32,384,128]{2,1,0:T(8,128)(2,1)}), bf16[32,384,128]{2,1,0:T(8,128)(2,1)S(1)}, u32[]{:S(2)}, u32[]{:S(2)}) async-start(bf16[32,384,128]{2,1,0:T(8,128)(2,1)} %encode_bulk.1.refs_0_), calls=%async_computation | async-start | bytes 6291456 | tf_op jit(solution)/shard_map/all_to_all | solution.py:557
  25.8 5.6 %encode_head.3 = (bf16[2,4,192,128]{3,2,1,0:T(8,128)(2,1)}, bf16[2,4,192,128]{3,2,1,0:T(8,128)(2,1)}, bf16[2,4,192,128]{3,2,1,0:T(8,128)(2,1)}, bf16[2,4,192,128...) custom-call(bf16[32,384,128]{2,1,0:T(8,128)(2,1)} %encode_bulk.1.ref, ...), custom_call_target="tpu_custom_call" | custom-call | tf_op jit(solution)/shard_map/encode_head/pallas_call | solution.py:210
  31.4 0.0 collective-permute-done.3.refs_5_
  31.4 1.6 collective-permute-start.16
  33.0 0.0 collective-permute-done.4.refs_6_
  33.0 0.6 collective-permute-start.2
  33.5 2.8 %collective-permute-start.17 = (bf16[2,4,176,128]{3,2,1,0:T(8,128)(2,1)}, bf16[2,4,176,128]{3,2,1,0:T(8,128)(2,1)}, u32[]{:S(2)}, u32[]{:S(2)}) collective-permute-start(bf16[2,4,176,128]{3,2,1,0:T(8,128)(2,1)} %get-tuple-element.70), channel_id=1, source_target_pairs={{0,16},{8,24},{16,0},{24,8},{1,17},{9,25},{17,1},{25,9},{2,18},{10... | collective-permute-start | bytes 1081352 | tf_op jit(solution)/shard_map/ppermute | solution.py:532
  36.3 34.9 %collective-permute-done.16.refs_5_ = bf16[2,4,176,128]{3,2,1,0:T(8,128)(2,1)S(1)} collective-permute-done((bf16[2,4,176,128]{3,2,1,0:T(8,128)(2,1)}, bf16[2,4,176,128]{3,2,1,0:T(8,128)(2,1)S(1)}, u32[]{:S(2)}, u32[]{:S(2)}) %collective-permute-start.16) | collective-permute-done | bytes 360480 | tf_op jit(solution)/shard_map/ppermute | solution.py:532
  71.2 1.1 collective-permute-start.13
  72.3 0.0 collective-permute-done.refs_1_
  72.3 1.2 collective-permute-start.14
  73.5 1.0 collective-permute-start.15
  74.5 0.0 collective-permute-done.2.refs_3_
  74.5 2.2 %collective-permute-start.18 = (bf16[2,4,176,128]{3,2,1,0:T(8,128)(2,1)}, bf16[2,4,176,128]{3,2,1,0:T(8,128)(2,1)}, u32[]{:S(2)}, u32[]{:S(2)}) collective-permute-start(bf16[2,4,176,128]{3,2,1,0:T(8,128)(2,1)} %get-tuple-element.71), channel_id=1, source_target_pairs={{0,24},{8,0},{16,8},{24,16},{1,25},{9,1},{17,9},{25,17},{2,26},{10... | collective-permute-start | bytes 1081352 | tf_op jit(solution)/shard_map/ppermute | solution.py:532
  76.7 2.4 %sifted.2 = bf16[4,4,368,128]{3,2,1,0:T(8,128)(2,1)} custom-call(bf16[2,4,192,128]{3,2,1,0:T(8,128)(2,1)} %get-tuple-element.46.refs_0_, bf16[2,4,192,128]{3,2,1,0:T(8,128)(2,1)} %copy-done.1, bf16[2,4,192,128]{3,2,1,0:T(8,128)(2,1)} %collective-permute-done.1.refs_2_, bf16[2,4,192,128]{3,2,1,0:T(8,128)(2,1)} %collective-permute-done.2.refs_3_, ...), custom_call_target="tpu_custom_call" | custom-call | tf_op jit(solution)/shard_map/sifted/pallas_call | solution.py:243
  79.1 0.1 collective-permute-done.17.refs_6_
  79.2 0.0 collective-permute-start.6
  79.2 5.0 %collective-permute-done.18.refs_7_ = bf16[2,4,176,128]{3,2,1,0:T(8,128)(2,1)} collective-permute-done((bf16[2,4,176,128]{3,2,1,0:T(8,128)(2,1)}, bf16[2,4,176,128]{3,2,1,0:T(8,128)(2,1)}, u32[]{:S(2)}, u32[]{:S(2)}) %collective-permute-start.18) | collective-permute-done | bytes 360480 | tf_op jit(solution)/shard_map/ppermute | solution.py:532
  84.2 6.5 %collective-permute-done.13.refs_1_ = bf16[2,4,192,128]{3,2,1,0:T(8,128)(2,1)} collective-permute-done((bf16[2,4,192,128]{3,2,1,0:T(8,128)(2,1)}, bf16[2,4,192,128]{3,2,1,0:T(8,128)(2,1)}, u32[]{:S(2)}, u32[]{:S(2)}) %collective-permute-start.13) | collective-permute-done | bytes 393248 | tf_op jit(solution)/shard_map/ppermute | solution.py:532
  90.7 0.0 collective-permute-done.14.refs_2_
  90.7 1.9 %collective-permute-done.15.refs_3_ = bf16[2,4,192,128]{3,2,1,0:T(8,128)(2,1)} collective-permute-done((bf16[2,4,192,128]{3,2,1,0:T(8,128)(2,1)}, bf16[2,4,192,128]{3,2,1,0:T(8,128)(2,1)}, u32[]{:S(2)}, u32[]{:S(2)}) %collective-permute-start.15) | collective-permute-done | bytes 393248 | tf_op jit(solution)/shard_map/ppermute | solution.py:532
  92.6 2.4 %sifted.3 = bf16[4,4,368,128]{3,2,1,0:T(8,128)(2,1)} custom-call(bf16[2,4,192,128]{3,2,1,0:T(8,128)(2,1)} %get-tuple-element.64.refs_0_, bf16[2,4,192,128]{3,2,1,0:T(8,128)(2,1)} %collective-permute-done.13.refs_1_, bf16[2,4,192,128]{3,2,1,0:T(8,128)(2,1)} %collective-permute-done.14.refs_2_, bf16[2,4,192,128]{3,2,1,0:T(8,128)(2,1)} %collective-permute-done.15.refs_3_, ...), custom_call_target="tpu_custom_call" | custom-call | tf_op jit(solution)/shard_map/sifted/pallas_call | solution.py:243
  95.0 0.1 collective-permute-start.19
  95.1 0.0 collective-permute-done.6.got
  95.1 3.1 %crossed.2 = (bf16[2,4,192,128]{3,2,1,0:T(8,128)(2,1)}, bf16[2,4,192,128]{3,2,1,0:T(8,128)(2,1)}, bf16[2,4,192,128]{3,2,1,0:T(8,128)(2,1)}, bf16[2,4,192,128]{3,...) custom-call(bf16[4,4,368,128]{3,2,1,0:T(8,128)(2,1)} %collective-per, ...), custom_call_target="tpu_custom_call" | custom-call | tf_op jit(solution)/shard_map/crossed/pallas_call | solution.py:274
  98.2 1.4 collective-permute-start.10
  99.5 1.1 collective-permute-start.11
  100.7 0.9 collective-permute-start.12
  101.6 3.1 %crossed.3 = (bf16[2,4,192,128]{3,2,1,0:T(8,128)(2,1)}, bf16[2,4,192,128]{3,2,1,0:T(8,128)(2,1)}, bf16[2,4,192,128]{3,2,1,0:T(8,128)(2,1)}, bf16[2,4,192,128]{3,...) custom-call(bf16[4,4,368,128]{3,2,1,0:T(8,128)(2,1)} %collective-per, ...), custom_call_target="tpu_custom_call" | custom-call | tf_op jit(solution)/shard_map/crossed/pallas_call | solution.py:274
  104.7 1.2 collective-permute-start.23
  105.9 2.4 %collective-permute-start.24 = (bf16[2,4,176,128]{3,2,1,0:T(8,128)(2,1)}, bf16[2,4,176,128]{3,2,1,0:T(8,128)(2,1)S(1)}, u32[]{:S(2)}, u32[]{:S(2)}) collective-permute-start(bf16[2,4,176,128]{3,2,1,0:T(8,128)(2,1)} %get-tuple-element.78), channel_id=1, source_target_pairs={{0,4},{2,6},{4,0},{6,2},{1,5},{3,7},{5,1},{7,3},{8,12},{10,14},{12... | collective-permute-start | bytes 1081352 | tf_op jit(solution)/shard_map/ppermute | solution.py:532
  108.3 2.0 %collective-permute-done.10.refs_5_ = bf16[2,4,176,128]{3,2,1,0:T(8,128)(2,1)S(1)} collective-permute-done((bf16[2,4,176,128]{3,2,1,0:T(8,128)(2,1)}, bf16[2,4,176,128]{3,2,1,0:T(8,128)(2,1)S(1)}, u32[]{:S(2)}, u32[]{:S(2)}) %collective-permute-start.10) | collective-permute-done | bytes 360480 | tf_op jit(solution)/shard_map/ppermute | solution.py:532
  110.2 0.7 copy-done.4
  111.0 0.0 collective-permute-start.7
  111.0 7.0 %collective-permute-done.11.refs_6_ = bf16[2,4,176,128]{3,2,1,0:T(8,128)(2,1)} collective-permute-done((bf16[2,4,176,128]{3,2,1,0:T(8,128)(2,1)}, bf16[2,4,176,128]{3,2,1,0:T(8,128)(2,1)}, u32[]{:S(2)}, u32[]{:S(2)}) %collective-permute-start.11) | collective-permute-done | bytes 360480 | tf_op jit(solution)/shard_map/ppermute | solution.py:532
  118.0 0.0 collective-permute-start.25
  118.0 1.7 collective-permute-done.12.refs_7_
  119.7 0.6 collective-permute-start.8
  120.3 4.4 %collective-permute-done.23.refs_5_ = bf16[2,4,176,128]{3,2,1,0:T(8,128)(2,1)S(1)} collective-permute-done((bf16[2,4,176,128]{3,2,1,0:T(8,128)(2,1)}, bf16[2,4,176,128]{3,2,1,0:T(8,128)(2,1)S(1)}, u32[]{:S(2)}, u32[]{:S(2)}) %collective-permute-start.23) | collective-permute-done | bytes 360480 | tf_op jit(solution)/shard_map/ppermute | solution.py:532
  124.7 1.1 collective-permute-start.9
  125.9 7.0 %collective-permute-done.24.refs_6_ = bf16[2,4,176,128]{3,2,1,0:T(8,128)(2,1)S(1)} collective-permute-done((bf16[2,4,176,128]{3,2,1,0:T(8,128)(2,1)}, bf16[2,4,176,128]{3,2,1,0:T(8,128)(2,1)S(1)}, u32[]{:S(2)}, u32[]{:S(2)}) %collective-permute-start.24) | collective-permute-done | bytes 360480 | tf_op jit(solution)/shard_map/ppermute | solution.py:532
  132.9 0.0 collective-permute-start.20
  132.9 1.4 collective-permute-done.25.refs_7_
  134.3 1.4 collective-permute-start.21
  135.7 1.1 collective-permute-start.22
  136.9 1.6 copy-done
  138.5 5.9 %decode_bulk.1 = (bf16[44,16,2048]{2,1,0:T(8,128)(2,1)}, f32[16,44]{1,0:T(8,128)}, bf16[16,2048]{1,0:T(8,128)(2,1)}) custom-call(bf16[16,2,384,128]{3,2,1,0:T(8,128)(2,1)} %bitcast.8), custom_call_target="tpu_custom_call" | custom-call | tf_op jit(solution)/shard_map/decode_bulk/pallas_call | solution.py:422
  144.4 2.0 %collective-permute-start.26 = (bf16[16,2048]{1,0:T(8,128)(2,1)}, bf16[16,2048]{1,0:T(8,128)(2,1)S(1)}, u32[]{:S(2)}, u32[]{:S(2)}) collective-permute-start(bf16[16,2048]{1,0:T(8,128)(2,1)} %get-tuple-element.84.refs_0_), channel_id=1, source_target_pairs={{0,32},{32,64},{64,96},{96,0},{1,33},{33,65},{65,97},{97,1},{2,34}... | collective-permute-start | bytes 196616 | tf_op jit(solution)/shard_map/ppermute | solution.py:532
  146.4 3.6 %collective-permute-start.27 = (bf16[16,2048]{1,0:T(8,128)(2,1)}, bf16[16,2048]{1,0:T(8,128)(2,1)S(1)}, u32[]{:S(2)}, u32[]{:S(2)}) collective-permute-start(bf16[16,2048]{1,0:T(8,128)(2,1)} %get-tuple-element.84.refs_0_), channel_id=1, source_target_pairs={{0,64},{32,96},{64,0},{96,32},{1,65},{33,97},{65,1},{97,33},{2,66}... | collective-permute-start | bytes 196616 | tf_op jit(solution)/shard_map/ppermute | solution.py:532
  150.0 3.4 %collective-permute-done.20.refs_1_ = bf16[2,4,192,128]{3,2,1,0:T(8,128)(2,1)} collective-permute-done((bf16[2,4,192,128]{3,2,1,0:T(8,128)(2,1)}, bf16[2,4,192,128]{3,2,1,0:T(8,128)(2,1)}, u32[]{:S(2)}, u32[]{:S(2)}) %collective-permute-start.20) | collective-permute-done | bytes 393248 | tf_op jit(solution)/shard_map/ppermute | solution.py:532
  153.5 4.0 %collective-permute-start.28 = (bf16[16,2048]{1,0:T(8,128)(2,1)}, bf16[16,2048]{1,0:T(8,128)(2,1)S(1)}, u32[]{:S(2)}, u32[]{:S(2)}) collective-permute-start(bf16[16,2048]{1,0:T(8,128)(2,1)} %get-tuple-element.84.refs_0_), channel_id=1, source_target_pairs={{0,96},{32,0},{64,32},{96,64},{1,97},{33,1},{65,33},{97,65},{2,98}... | collective-permute-start | bytes 196616 | tf_op jit(solution)/shard_map/ppermute | solution.py:532
  157.5 5.7 %decode_head.2 = (bf16[44,16,2048]{2,1,0:T(8,128)(2,1)}, f32[16,44]{1,0:T(8,128)}) custom-call(bf16[2,4,192,128]{3,2,1,0:T(8,128)(2,1)} %get-tuple-element.54.refs_0_, bf16[2,4,192,128]{3,2,1,0:T(8,128)(2,1)} %copy-done.3, bf16[2,4,192,128]{3,2,1,0:T(8,128)(2,1)} %collective-permute-done.8.refs_2_, bf16[2,4,192,128]{3,2,1,0:T(8,128)(2,1)} %collective-permute-done.9.refs_3_, ...), custom_call_target="tpu_custom_call" | custom-call | tf_op jit(solution)/shard_map/decode_head/pallas_call | solution.py:494
  163.2 5.7 %decode_head.3 = (bf16[44,16,2048]{2,1,0:T(8,128)(2,1)}, f32[16,44]{1,0:T(8,128)}) custom-call(bf16[2,4,192,128]{3,2,1,0:T(8,128)(2,1)} %get-tuple-element.72.refs_0_, bf16[2,4,192,128]{3,2,1,0:T(8,128)(2,1)} %collective-permute-done.20.refs_1_, bf16[2,4,192,128]{3,2,1,0:T(8,128)(2,1)} %collective-permute-done.21.refs_2_, ...), custom_call_target="tpu_custom_call" | custom-call | tf_op jit(solution)/shard_map/decode_head/pallas_call | solution.py:494
  169.0 0.6 copy-done.8
  169.6 0.0 copy-done.9
  169.6 0.6 copy-done.10
  170.2 1.7 joined.1
  (29 shorter events, 0.1 us)
Async XLA Ops:
  6.2 25.1 %collective-permute-start.3 = (bf16[2,4,176,128]{3,2,1,0:T(8,128)(2,1)}, bf16[2,4,176,128]{3,2,1,0:T(8,128)(2,1)}, u32[]{:S(2)}, u32[]{:S(2)}) collective-permute-start(bf16[2,4,176,128]{3,2,1,0:T(8,128)(2,1)} %get-tuple-element.51), channel_id=1, source_target_pairs={{0,8},{8,16},{16,24},{24,0},{1,9},{9,17},{17,25},{25,1},{2,10},{10... | collective-permute-start | bytes 1081352 | tf_op jit(solution)/shard_map/ppermute | solution.py:532
  7.9 25.1 %collective-permute-start.4 = (bf16[2,4,176,128]{3,2,1,0:T(8,128)(2,1)}, bf16[2,4,176,128]{3,2,1,0:T(8,128)(2,1)}, u32[]{:S(2)}, u32[]{:S(2)}) collective-permute-start(bf16[2,4,176,128]{3,2,1,0:T(8,128)(2,1)} %get-tuple-element.52), channel_id=1, source_target_pairs={{0,16},{8,24},{16,0},{24,8},{1,17},{9,25},{17,1},{25,9},{2,18},{10... | collective-permute-start | bytes 1081352 | tf_op jit(solution)/shard_map/ppermute | solution.py:532
  10.8 22.7 %collective-permute-start.5 = (bf16[2,4,176,128]{3,2,1,0:T(8,128)(2,1)}, bf16[2,4,176,128]{3,2,1,0:T(8,128)(2,1)}, u32[]{:S(2)}, u32[]{:S(2)}) collective-permute-start(bf16[2,4,176,128]{3,2,1,0:T(8,128)(2,1)} %get-tuple-element.53), channel_id=1, source_target_pairs={{0,24},{8,0},{16,8},{24,16},{1,25},{9,1},{17,9},{25,17},{2,26},{10... | collective-permute-start | bytes 1081352 | tf_op jit(solution)/shard_map/ppermute | solution.py:532
  12.1 60.2 %collective-permute-start = (bf16[2,4,192,128]{3,2,1,0:T(8,128)(2,1)}, bf16[2,4,192,128]{3,2,1,0:T(8,128)(2,1)S(1)}, u32[]{:S(2)}, u32[]{:S(2)}) collective-permute-start(bf16[2,4,192,128]{3,2,1,0:T(8,128)(2,1)} %get-tuple-element.47), channel_id=1, source_target_pairs={{0,2},{2,4},{4,6},{6,0},{1,3},{3,5},{5,7},{7,1},{8,10},{10,12},{12... | collective-permute-start | bytes 1179656 | tf_op jit(solution)/shard_map/ppermute | solution.py:532
  13.3 60.2 %collective-permute-start.1 = (bf16[2,4,192,128]{3,2,1,0:T(8,128)(2,1)}, bf16[2,4,192,128]{3,2,1,0:T(8,128)(2,1)}, u32[]{:S(2)}, u32[]{:S(2)}) collective-permute-start(bf16[2,4,192,128]{3,2,1,0:T(8,128)(2,1)} %get-tuple-element.48), channel_id=1, source_target_pairs={{0,4},{2,6},{4,0},{6,2},{1,5},{3,7},{5,1},{7,3},{8,12},{10,14},{12... | collective-permute-start | bytes 1179656 | tf_op jit(solution)/shard_map/ppermute | solution.py:532
  19.3 117.6 %all-to-all-start = ((bf16[32,384,128]{2,1,0:T(8,128)(2,1)}), bf16[32,384,128]{2,1,0:T(8,128)(2,1)S(1)}, u32[]{:S(2)}, u32[]{:S(2)}) async-start(bf16[32,384,128]{2,1,0:T(8,128)(2,1)} %encode_bulk.1.refs_0_), calls=%async_computation | async-start | bytes 6291456 | tf_op jit(solution)/shard_map/all_to_all | solution.py:557
  31.4 39.8 %collective-permute-start.16 = (bf16[2,4,176,128]{3,2,1,0:T(8,128)(2,1)}, bf16[2,4,176,128]{3,2,1,0:T(8,128)(2,1)S(1)}, u32[]{:S(2)}, u32[]{:S(2)}) collective-permute-start(bf16[2,4,176,128]{3,2,1,0:T(8,128)(2,1)} %get-tuple-element.69), channel_id=1, source_target_pairs={{0,8},{8,16},{16,24},{24,0},{1,9},{9,17},{17,25},{25,1},{2,10},{10... | collective-permute-start | bytes 1081352 | tf_op jit(solution)/shard_map/ppermute | solution.py:532
  33.0 41.6 %collective-permute-start.2 = (bf16[2,4,192,128]{3,2,1,0:T(8,128)(2,1)}, bf16[2,4,192,128]{3,2,1,0:T(8,128)(2,1)}, u32[]{:S(2)}, u32[]{:S(2)}) collective-permute-start(bf16[2,4,192,128]{3,2,1,0:T(8,128)(2,1)} %get-tuple-element.49), channel_id=1, source_target_pairs={{0,6},{2,0},{4,2},{6,4},{1,7},{3,1},{5,3},{7,5},{8,14},{10,8},{12,... | collective-permute-start | bytes 1179656 | tf_op jit(solution)/shard_map/ppermute | solution.py:532
  33.5 45.7 %collective-permute-start.17 = (bf16[2,4,176,128]{3,2,1,0:T(8,128)(2,1)}, bf16[2,4,176,128]{3,2,1,0:T(8,128)(2,1)}, u32[]{:S(2)}, u32[]{:S(2)}) collective-permute-start(bf16[2,4,176,128]{3,2,1,0:T(8,128)(2,1)} %get-tuple-element.70), channel_id=1, source_target_pairs={{0,16},{8,24},{16,0},{24,8},{1,17},{9,25},{17,1},{25,9},{2,18},{10... | collective-permute-start | bytes 1081352 | tf_op jit(solution)/shard_map/ppermute | solution.py:532
  71.2 1.1 copy-start.2
  71.2 19.5 %collective-permute-start.13 = (bf16[2,4,192,128]{3,2,1,0:T(8,128)(2,1)}, bf16[2,4,192,128]{3,2,1,0:T(8,128)(2,1)}, u32[]{:S(2)}, u32[]{:S(2)}) collective-permute-start(bf16[2,4,192,128]{3,2,1,0:T(8,128)(2,1)} %get-tuple-element.65), channel_id=1, source_target_pairs={{0,2},{2,4},{4,6},{6,0},{1,3},{3,5},{5,7},{7,1},{8,10},{10,12},{12... | collective-permute-start | bytes 1179656 | tf_op jit(solution)/shard_map/ppermute | solution.py:532
  72.3 4.4 %copy-start.1 = (bf16[2,4,192,128]{3,2,1,0:T(8,128)(2,1)}, bf16[2,4,192,128]{3,2,1,0:T(8,128)(2,1)S(1)}, u32[]{:S(2)}) copy-start(bf16[2,4,192,128]{3,2,1,0:T(8,128)(2,1)S(1)} %collective-permute-done.refs_1_) | copy-start | bytes 1179652
  72.3 18.4 %collective-permute-start.14 = (bf16[2,4,192,128]{3,2,1,0:T(8,128)(2,1)}, bf16[2,4,192,128]{3,2,1,0:T(8,128)(2,1)}, u32[]{:S(2)}, u32[]{:S(2)}) collective-permute-start(bf16[2,4,192,128]{3,2,1,0:T(8,128)(2,1)} %get-tuple-element.66), channel_id=1, source_target_pairs={{0,4},{2,6},{4,0},{6,2},{1,5},{3,7},{5,1},{7,3},{8,12},{10,14},{12... | collective-permute-start | bytes 1179656 | tf_op jit(solution)/shard_map/ppermute | solution.py:532
  73.5 19.1 %collective-permute-start.15 = (bf16[2,4,192,128]{3,2,1,0:T(8,128)(2,1)}, bf16[2,4,192,128]{3,2,1,0:T(8,128)(2,1)}, u32[]{:S(2)}, u32[]{:S(2)}) collective-permute-start(bf16[2,4,192,128]{3,2,1,0:T(8,128)(2,1)} %get-tuple-element.67), channel_id=1, source_target_pairs={{0,6},{2,0},{4,2},{6,4},{1,7},{3,1},{5,3},{7,5},{8,14},{10,8},{12,... | collective-permute-start | bytes 1179656 | tf_op jit(solution)/shard_map/ppermute | solution.py:532
  74.5 9.6 %collective-permute-start.18 = (bf16[2,4,176,128]{3,2,1,0:T(8,128)(2,1)}, bf16[2,4,176,128]{3,2,1,0:T(8,128)(2,1)}, u32[]{:S(2)}, u32[]{:S(2)}) collective-permute-start(bf16[2,4,176,128]{3,2,1,0:T(8,128)(2,1)} %get-tuple-element.71), channel_id=1, source_target_pairs={{0,24},{8,0},{16,8},{24,16},{1,25},{9,1},{17,9},{25,17},{2,26},{10... | collective-permute-start | bytes 1081352 | tf_op jit(solution)/shard_map/ppermute | solution.py:532
  79.2 15.9 %collective-permute-start.6 = (bf16[4,4,368,128]{3,2,1,0:T(8,128)(2,1)}, bf16[4,4,368,128]{3,2,1,0:T(8,128)(2,1)}, u32[]{:S(2)}, u32[]{:S(2)}) collective-permute-start(bf16[4,4,368,128]{3,2,1,0:T(8,128)(2,1)} %sifted.2), channel_id=1, source_target_pairs={{0,1},{1,0},{2,3},{3,2},{4,5},{5,4},{6,7},{7,6},{8,9},{9,8},{10,11... | collective-permute-start | bytes 4521992 | tf_op jit(solution)/shard_map/ppermute | solution.py:551
  95.0 6.6 %collective-permute-start.19 = (bf16[4,4,368,128]{3,2,1,0:T(8,128)(2,1)}, bf16[4,4,368,128]{3,2,1,0:T(8,128)(2,1)}, u32[]{:S(2)}, u32[]{:S(2)}) collective-permute-start(bf16[4,4,368,128]{3,2,1,0:T(8,128)(2,1)} %sifted.3), channel_id=1, source_target_pairs={{0,1},{1,0},{2,3},{3,2},{4,5},{5,4},{6,7},{7,6},{8,9},{9,8},{10,11... | collective-permute-start | bytes 4521992 | tf_op jit(solution)/shard_map/ppermute | solution.py:551
  98.2 12.1 %collective-permute-start.10 = (bf16[2,4,176,128]{3,2,1,0:T(8,128)(2,1)}, bf16[2,4,176,128]{3,2,1,0:T(8,128)(2,1)S(1)}, u32[]{:S(2)}, u32[]{:S(2)}) collective-permute-start(bf16[2,4,176,128]{3,2,1,0:T(8,128)(2,1)} %get-tuple-element.59), channel_id=1, source_target_pairs={{0,2},{2,4},{4,6},{6,0},{1,3},{3,5},{5,7},{7,1},{8,10},{10,12},{12... | collective-permute-start | bytes 1081352 | tf_op jit(solution)/shard_map/ppermute | solution.py:532
  99.5 18.5 %collective-permute-start.11 = (bf16[2,4,176,128]{3,2,1,0:T(8,128)(2,1)}, bf16[2,4,176,128]{3,2,1,0:T(8,128)(2,1)}, u32[]{:S(2)}, u32[]{:S(2)}) collective-permute-start(bf16[2,4,176,128]{3,2,1,0:T(8,128)(2,1)} %get-tuple-element.60), channel_id=1, source_target_pairs={{0,4},{2,6},{4,0},{6,2},{1,5},{3,7},{5,1},{7,3},{8,12},{10,14},{12... | collective-permute-start | bytes 1081352 | tf_op jit(solution)/shard_map/ppermute | solution.py:532
  100.7 19.0 %collective-permute-start.12 = (bf16[2,4,176,128]{3,2,1,0:T(8,128)(2,1)}, bf16[2,4,176,128]{3,2,1,0:T(8,128)(2,1)}, u32[]{:S(2)}, u32[]{:S(2)}) collective-permute-start(bf16[2,4,176,128]{3,2,1,0:T(8,128)(2,1)} %get-tuple-element.61), channel_id=1, source_target_pairs={{0,6},{2,0},{4,2},{6,4},{1,7},{3,1},{5,3},{7,5},{8,14},{10,8},{12,... | collective-permute-start | bytes 1081352 | tf_op jit(solution)/shard_map/ppermute | solution.py:532
  104.7 20.0 %collective-permute-start.23 = (bf16[2,4,176,128]{3,2,1,0:T(8,128)(2,1)}, bf16[2,4,176,128]{3,2,1,0:T(8,128)(2,1)S(1)}, u32[]{:S(2)}, u32[]{:S(2)}) collective-permute-start(bf16[2,4,176,128]{3,2,1,0:T(8,128)(2,1)} %get-tuple-element.77), channel_id=1, source_target_pairs={{0,2},{2,4},{4,6},{6,0},{1,3},{3,5},{5,7},{7,1},{8,10},{10,12},{12... | collective-permute-start | bytes 1081352 | tf_op jit(solution)/shard_map/ppermute | solution.py:532
  105.9 27.0 %collective-permute-start.24 = (bf16[2,4,176,128]{3,2,1,0:T(8,128)(2,1)}, bf16[2,4,176,128]{3,2,1,0:T(8,128)(2,1)S(1)}, u32[]{:S(2)}, u32[]{:S(2)}) collective-permute-start(bf16[2,4,176,128]{3,2,1,0:T(8,128)(2,1)} %get-tuple-element.78), channel_id=1, source_target_pairs={{0,4},{2,6},{4,0},{6,2},{1,5},{3,7},{5,1},{7,3},{8,12},{10,14},{12... | collective-permute-start | bytes 1081352 | tf_op jit(solution)/shard_map/ppermute | solution.py:532
  110.2 0.7 copy-start.4
  111.0 24.7 %collective-permute-start.7 = (bf16[2,4,192,128]{3,2,1,0:T(8,128)(2,1)}, bf16[2,4,192,128]{3,2,1,0:T(8,128)(2,1)S(1)}, u32[]{:S(2)}, u32[]{:S(2)}) collective-permute-start(bf16[2,4,192,128]{3,2,1,0:T(8,128)(2,1)} %get-tuple-element.55), channel_id=1, source_target_pairs={{0,8},{8,16},{16,24},{24,0},{1,9},{9,17},{17,25},{25,1},{2,10},{10... | collective-permute-start | bytes 1179656 | tf_op jit(solution)/shard_map/ppermute | solution.py:532
  118.0 16.3 %collective-permute-start.25 = (bf16[2,4,176,128]{3,2,1,0:T(8,128)(2,1)}, bf16[2,4,176,128]{3,2,1,0:T(8,128)(2,1)S(1)}, u32[]{:S(2)}, u32[]{:S(2)}) collective-permute-start(bf16[2,4,176,128]{3,2,1,0:T(8,128)(2,1)} %get-tuple-element.79), channel_id=1, source_target_pairs={{0,6},{2,0},{4,2},{6,4},{1,7},{3,1},{5,3},{7,5},{8,14},{10,8},{12,... | collective-permute-start | bytes 1081352 | tf_op jit(solution)/shard_map/ppermute | solution.py:532
  119.7 24.8 %collective-permute-start.8 = (bf16[2,4,192,128]{3,2,1,0:T(8,128)(2,1)}, bf16[2,4,192,128]{3,2,1,0:T(8,128)(2,1)}, u32[]{:S(2)}, u32[]{:S(2)}) collective-permute-start(bf16[2,4,192,128]{3,2,1,0:T(8,128)(2,1)} %get-tuple-element.56), channel_id=1, source_target_pairs={{0,16},{8,24},{16,0},{24,8},{1,17},{9,25},{17,1},{25,9},{2,18},{10... | collective-permute-start | bytes 1179656 | tf_op jit(solution)/shard_map/ppermute | solution.py:532
  124.7 11.0 %copy-start.5 = (bf16[2,4,176,128]{3,2,1,0:T(8,128)(2,1)}, bf16[2,4,176,128]{3,2,1,0:T(8,128)(2,1)S(1)}, u32[]{:S(2)}) copy-start(bf16[2,4,176,128]{3,2,1,0:T(8,128)(2,1)S(1)} %collective-permute-done.23.refs_5_) | copy-start | bytes 1081348
  124.7 21.7 %collective-permute-start.9 = (bf16[2,4,192,128]{3,2,1,0:T(8,128)(2,1)}, bf16[2,4,192,128]{3,2,1,0:T(8,128)(2,1)}, u32[]{:S(2)}, u32[]{:S(2)}) collective-permute-start(bf16[2,4,192,128]{3,2,1,0:T(8,128)(2,1)} %get-tuple-element.57), channel_id=1, source_target_pairs={{0,24},{8,0},{16,8},{24,16},{1,25},{9,1},{17,9},{25,17},{2,26},{10... | collective-permute-start | bytes 1179656 | tf_op jit(solution)/shard_map/ppermute | solution.py:532
  132.9 2.8 %copy-start.6 = (bf16[2,4,176,128]{3,2,1,0:T(8,128)(2,1)}, bf16[2,4,176,128]{3,2,1,0:T(8,128)(2,1)S(1)}, u32[]{:S(2)}) copy-start(bf16[2,4,176,128]{3,2,1,0:T(8,128)(2,1)S(1)} %collective-permute-done.24.refs_6_) | copy-start | bytes 1081348
  132.9 20.6 %collective-permute-start.20 = (bf16[2,4,192,128]{3,2,1,0:T(8,128)(2,1)}, bf16[2,4,192,128]{3,2,1,0:T(8,128)(2,1)}, u32[]{:S(2)}, u32[]{:S(2)}) collective-permute-start(bf16[2,4,192,128]{3,2,1,0:T(8,128)(2,1)} %get-tuple-element.73), channel_id=1, source_target_pairs={{0,8},{8,16},{16,24},{24,0},{1,9},{9,17},{17,25},{25,1},{2,10},{10... | collective-permute-start | bytes 1179656 | tf_op jit(solution)/shard_map/ppermute | solution.py:532
  134.3 1.4 copy-start.7
  134.3 28.9 %collective-permute-start.21 = (bf16[2,4,192,128]{3,2,1,0:T(8,128)(2,1)}, bf16[2,4,192,128]{3,2,1,0:T(8,128)(2,1)}, u32[]{:S(2)}, u32[]{:S(2)}) collective-permute-start(bf16[2,4,192,128]{3,2,1,0:T(8,128)(2,1)} %get-tuple-element.74), channel_id=1, source_target_pairs={{0,16},{8,24},{16,0},{24,8},{1,17},{9,25},{17,1},{25,9},{2,18},{10... | collective-permute-start | bytes 1179656 | tf_op jit(solution)/shard_map/ppermute | solution.py:532
  135.7 21.8 %copy-start.3 = (bf16[2,4,192,128]{3,2,1,0:T(8,128)(2,1)}, bf16[2,4,192,128]{3,2,1,0:T(8,128)(2,1)S(1)}, u32[]{:S(2)}) copy-start(bf16[2,4,192,128]{3,2,1,0:T(8,128)(2,1)S(1)} %collective-permute-done.7.refs_1_) | copy-start | bytes 1179652
  135.7 27.5 %collective-permute-start.22 = (bf16[2,4,192,128]{3,2,1,0:T(8,128)(2,1)}, bf16[2,4,192,128]{3,2,1,0:T(8,128)(2,1)}, u32[]{:S(2)}, u32[]{:S(2)}) collective-permute-start(bf16[2,4,192,128]{3,2,1,0:T(8,128)(2,1)} %get-tuple-element.75), channel_id=1, source_target_pairs={{0,24},{8,0},{16,8},{24,16},{1,25},{9,1},{17,9},{25,17},{2,26},{10... | collective-permute-start | bytes 1179656 | tf_op jit(solution)/shard_map/ppermute | solution.py:532
  136.9 1.6 copy-start
  144.4 24.5 %collective-permute-start.26 = (bf16[16,2048]{1,0:T(8,128)(2,1)}, bf16[16,2048]{1,0:T(8,128)(2,1)S(1)}, u32[]{:S(2)}, u32[]{:S(2)}) collective-permute-start(bf16[16,2048]{1,0:T(8,128)(2,1)} %get-tuple-element.84.refs_0_), channel_id=1, source_target_pairs={{0,32},{32,64},{64,96},{96,0},{1,33},{33,65},{65,97},{97,1},{2,34}... | collective-permute-start | bytes 196616 | tf_op jit(solution)/shard_map/ppermute | solution.py:532
  146.4 22.5 %collective-permute-start.27 = (bf16[16,2048]{1,0:T(8,128)(2,1)}, bf16[16,2048]{1,0:T(8,128)(2,1)S(1)}, u32[]{:S(2)}, u32[]{:S(2)}) collective-permute-start(bf16[16,2048]{1,0:T(8,128)(2,1)} %get-tuple-element.84.refs_0_), channel_id=1, source_target_pairs={{0,64},{32,96},{64,0},{96,32},{1,65},{33,97},{65,1},{97,33},{2,66}... | collective-permute-start | bytes 196616 | tf_op jit(solution)/shard_map/ppermute | solution.py:532
  153.5 15.5 %collective-permute-start.28 = (bf16[16,2048]{1,0:T(8,128)(2,1)}, bf16[16,2048]{1,0:T(8,128)(2,1)S(1)}, u32[]{:S(2)}, u32[]{:S(2)}) collective-permute-start(bf16[16,2048]{1,0:T(8,128)(2,1)} %get-tuple-element.84.refs_0_), channel_id=1, source_target_pairs={{0,96},{32,0},{64,32},{96,64},{1,97},{33,1},{65,33},{97,65},{2,98}... | collective-permute-start | bytes 196616 | tf_op jit(solution)/shard_map/ppermute | solution.py:532
  168.9 0.6 copy-start.8
  168.9 0.6 copy-start.9
  169.6 0.6 copy-start.10
